TPU v7x, 256 devices: a whole 4x4x8 slice. The times are simulated.
256 devices in a mesh: agent: 128 (over x, y, z), grid: 2 (over core).
Axes of the slice: x: 4, y: 4, z: 8, core: 2. Of those that a mesh axis runs over, the one named last changes fastest.
Arguments:
- value_prior: float32 [2048, 1024], P(None, 'agent'), may hold values from -6 to 6
- trans_weight: float32 [128, 128], replicated, may hold values from 0.05 to 1
- perceived_law_coefficient: float32 [4], replicated, may hold values from 0.7 to 1
- perceived_law_constant: float32 [4], replicated, may hold values from 0.5 to 4
- interest: float32 [4, 16], replicated, may hold values from 0 to 0.05
- wage_level: float32 [4, 16], replicated, may hold values from 0.5 to 1.5
- efficiency: float32 [32], replicated, may hold values from 0.2 to 3
- holdings: float32 [1048576], P('agent'), may hold values from 0 to 40
- shocks: int32 [4, 1048576], P(None, 'agent'), may hold values from 0 to 31
- brackets: int32 [4, 1048576], P(None, 'agent'), may hold values from 0 to 1022
- aggregate: int32 [4], replicated, may hold values from 0 to 3
Outputs:
- value_new: float32 [2048, 1024], P('agent', 'grid')
- policy: float32 [2048, 1024], P('agent', 'grid')
- holdings_final: float32 [1048576], P('agent')
- capital: float32 [4], replicated
All inputs are finite; a program needn't handle non-finite values.
Results may differ from a plain program's by a relative error of at most 0.0003.
Values sent between devices are 32-bit elements; how exact they have to be, the bound alone decides.
A program may use at most 64 MiB of HBM per device.

v0:
```python
import jax
import jax.numpy as jnp
from jax import lax
from jax.sharding import Mesh
from jax.sharding import PartitionSpec as P

A = 1024
E = 32
NK = 16
Z = 4
STATES = 2048
PERIODS = 4
AGENT = ("agent_0", "agent_1", "agent_2")


wealth_upper_limit = 40.0
beta_disc = 0.96
tau_soft = 0.02
floor_cons = 0.1
highest = lax.Precision.HIGHEST


def laid_out(parts, dim):
    parts = jnp.moveaxis(parts, 0, dim)
    shape = parts.shape
    return parts.reshape(*shape[:dim], shape[dim] * shape[dim + 1], *shape[dim + 2 :])


def sent_to_all(x, axis):
    copies = jnp.broadcast_to(x, (lax.axis_size(axis), *x.shape))
    return lax.all_to_all(copies, axis, split_axis=0, concat_axis=0, tiled=True)


def gathered_copies(x, axis, dim):
    return laid_out(sent_to_all(x, axis), dim)


def over_axes(x, axes):
    for axis in axes:
        x = lax.psum(x, axis)
    return x


def make_points():
    fraction = jnp.arange(A, dtype=jnp.float32) / (A - 1)
    return wealth_upper_limit * fraction * fraction


def hat_function_shares(position):
    spacing = wealth_upper_limit / (NK - 1)
    savings_mesh_points = wealth_upper_limit * jnp.arange(NK, dtype=jnp.float32) / (NK - 1)
    return jnp.maximum(0.0, 1.0 - jnp.abs(position[..., None] - savings_mesh_points) / spacing)


def one_hot(indices, number):
    return (indices[:, None] == jnp.arange(number, dtype=jnp.int32)[None, :]).astype(jnp.float32)


def state_parts(states):
    zone_of = states // (NK * E)
    level_of = states // E % NK
    kind_of = states % E
    return (zone_of, level_of, kind_of)


def expect_rows(rows_in, transition, offset_coefficients):
    columns = rows_in.shape[1]
    value_cube = rows_in.reshape(Z, NK, E, columns)
    blended = jnp.einsum(
        "zeyf,ykfn->zekn", transition.reshape(Z, E, Z, E), value_cube, precision=highest
    )
    result = jnp.einsum("zjk,zekn->zjen", offset_coefficients, blended, precision=highest)
    return result.reshape(STATES, columns)


def bellman(points, wealth, expected):
    consume = wealth[:, None] - points[None, :]
    clipped = jnp.maximum(consume, floor_cons)
    utility = jnp.log(clipped) + (consume - clipped) / floor_cons
    scores = (utility + beta_disc * expected[None, :]) / tau_soft
    highest_score = jnp.max(scores, axis=1, keepdims=True)
    weight = jnp.exp(scores - highest_score)
    totals = jnp.sum(weight, axis=1)
    values_now = tau_soft * (highest_score[:, 0] + jnp.log(totals))
    chosen = jnp.sum(weight * points[None, :], axis=1) / totals
    return (values_now, chosen)


def advance(lookup, points, current, shock_row, bracket_row):
    flattened = lookup.reshape(-1)
    flat_index = shock_row * lookup.shape[1] + bracket_row
    value_low = jnp.take(flattened, flat_index)
    value_high = jnp.take(flattened, flat_index + 1)
    edge_low = jnp.take(points, bracket_row)
    edge_high = jnp.take(points, bracket_row + 1)
    fraction = jnp.clip((current - edge_low) / (edge_high - edge_low), 0.0, 1.0)
    return value_low + fraction * (value_high - value_low)


def on_device(
    value_prior,
    trans_weight,
    perceived_law_coefficient,
    perceived_law_constant,
    interest,
    wage_level,
    efficiency,
    holdings,
    shocks,
    brackets,
    aggregate,
):
    agent_count = lax.axis_size(AGENT)
    per_device = STATES // agent_count
    half_rows = A // lax.axis_size("grid")
    first_state = lax.axis_index(AGENT) * per_device
    own_states = first_state + jnp.arange(per_device, dtype=jnp.int32)
    points = make_points()
    transition = trans_weight / jnp.sum(trans_weight, axis=1, keepdims=True)
    savings_mesh_points = wealth_upper_limit * jnp.arange(NK, dtype=jnp.float32) / (NK - 1)
    predicted_stock = jnp.clip(
        perceived_law_coefficient[:, None] * savings_mesh_points[None, :]
        + perceived_law_constant[:, None],
        0.0,
        wealth_upper_limit,
    )
    offset_coefficients = hat_function_shares(predicted_stock)
    partial_value = expect_rows(value_prior, transition, offset_coefficients)
    expected = lax.all_to_all(partial_value, AGENT, split_axis=0, concat_axis=1, tiled=True)
    zone_of, level_of, kind_of = state_parts(own_states)
    price_hot = one_hot(zone_of * NK + level_of, Z * NK)
    interest_own = jnp.sum(price_hot * interest.reshape(1, Z * NK), axis=1)
    wage_own = jnp.sum(price_hot * wage_level.reshape(1, Z * NK), axis=1)
    kind_hot = one_hot(kind_of, E)
    efficiency_own = jnp.sum(kind_hot * efficiency[None, :], axis=1)
    growth = 1.0 + interest_own
    income = wage_own * efficiency_own
    own_points = lax.dynamic_slice_in_dim(points, lax.axis_index("grid") * half_rows, half_rows)

    def one_state(packed):
        column, factor, earned = packed
        return bellman(points, own_points * factor + earned, column)

    values_now, policy = lax.map(one_state, (expected, growth, income))
    agents_total = holdings.shape[0] * agent_count
    halves_in = gathered_copies(policy, "grid", 1)
    policy_cube = lax.all_gather(halves_in, AGENT, axis=0, tiled=True).reshape(Z, NK, E, A)
    current = holdings
    capital_path = []
    for period in range(PERIODS):
        capital = over_axes(jnp.sum(current), AGENT) / agents_total
        capital_path.append(capital)
        knot_weights = hat_function_shares(capital)
        sliced = lax.dynamic_index_in_dim(policy_cube, aggregate[period], 0, keepdims=False)
        lookup = jnp.einsum("k,kea->ea", knot_weights, sliced, precision=highest)
        current = advance(lookup, points, current, shocks[period], brackets[period])
    return (values_now, policy, current, jnp.stack(capital_path))


def solution(mesh):
    finer = Mesh(
        mesh.devices.reshape(4, 4, 8, mesh.shape["grid"]), ("agent_0", "agent_1", "agent_2", "grid")
    )
    in_specs = (
        P(None, AGENT),
        P(),
        P(),
        P(),
        P(),
        P(),
        P(),
        P(AGENT),
        P(None, AGENT),
        P(None, AGENT),
        P(),
    )
    out_specs = (P(AGENT, "grid"), P(AGENT, "grid"), P(AGENT), P())
    return jax.shard_map(
        on_device, mesh=finer, in_specs=in_specs, out_specs=out_specs, check_vma=False
    )
```

profile of v0, /device:TPU:8, one launch (start us, length us, event | category | flops | bytes accessed | tf_op | source)
XLA Modules:
  0.0 961.3 jit_solution(12016140227608750191)
XLA Ops:
  13.5 15.3 %all-to-all-start = ((f32[128,1,128]{2,1,0:T(1,128)}), f32[128,1,128]{2,1,0:T(1,128)S(1)}, u32[]{:S(2)}, u32[]{:S(2)}) async-start(f32[128,1,128]{2,1,0:T(1,128)} %reshape.401), calls=%async_computation | async-start | bytes 131072 | tf_op jit(solution)/shard_map/all_to_all | solution.py:129
  29.6 10.3 %all-to-all-done = f32[128,1,128]{2,1,0:T(1,128)S(1)} async-done(((f32[128,1,128]{2,1,0:T(1,128)}), f32[128,1,128]{2,1,0:T(1,128)S(1)}, u32[]{:S(2)}, u32[]{:S(2)}) %all-to-all-start) | async-done | bytes 65568 | tf_op jit(solution)/shard_map/all_to_all | solution.py:129
  41.7 98.6 %while.14 = (s32[]{:T(128)}, f32[16,512]{1,0:T(8,128)}, f32[16,512]{1,0:T(8,128)S(1)}, f32[16]{0:T(128)S(1)}, f32[512]{0:T(512)S(1)}, /*index=5*/f32[16]{0:T(128)S(1)}, f32[16,1024]{1,0:T(8,128)S(1)}, s32[]{:T(128)}, s32[]{:T(128)}) while((s32[]{:T(128)}, f32[16,512]{1,0:T(8,128)}, f32[16,512]{1,0:T(8,128)S(1)}, ...), condition=%wide.region_8.9_spmd.clone.clone, body=%wide.region_4.8_spmd.clone.clone.sunk | while | flops 9966594 | bytes 63633 | solution.py:144
  145.4 9.0 psum.84
  154.4 9.8 %psum.85 = f32[]{:T(128)} all-reduce(f32[]{:T(128)} %psum.84), channel_id=1, replica_groups=mesh['agent_0'=4,'agent_1'=4,'agent_2'=8,'grid'=2] {'agent_1'}, use_global_device_ids=true, to_apply=%region_11.12 | all-reduce | flops 1 | bytes 8 | tf_op jit(solution)/shard_map/psum | solution.py:40
  164.2 15.9 %psum.86 = f32[]{:T(128)} all-reduce(f32[]{:T(128)} %psum.85), channel_id=1, replica_groups=mesh['agent_0'=4,'agent_1'=4,'agent_2'=8,'grid'=2] {'agent_2'}, use_global_device_ids=true, to_apply=%region_12.13 | all-reduce | flops 1 | bytes 8 | tf_op jit(solution)/shard_map/psum | solution.py:40
  186.2 32.9 %gather_fusion.2 = f32[8192]{0:T(1024)S(1)} fusion(f32[1024]{0:T(1024)S(1)} %fusion.55, s32[8192]{0:T(1024)S(1)} %get-tuple-element.165), kind=kCustom, calls=%fused_computation.9.clone | custom fusion | bytes 98304 | tf_op jit(solution)/shard_map/jit(_take)/gather | solution.py:95
  219.1 32.9 %gather_fusion.1 = f32[8192]{0:T(1024)S(1)} fusion(f32[1024]{0:T(1024)S(1)} %fusion.55, s32[8192]{0:T(1024)S(1)} %get-tuple-element.166), kind=kCustom, calls=%fused_computation.1.clone | custom fusion | bytes 98304 | tf_op jit(solution)/shard_map/jit(_take)/gather | solution.py:94
  252.1 32.9 %gather_fusion.6 = f32[8192]{0:T(1024)S(1)} fusion(f32[1024]{0:T(1024)S(1)} %fusion.55, s32[8192]{0:T(1024)S(1)} %get-tuple-element.163), kind=kCustom, calls=%fused_computation.11.clone | custom fusion | bytes 98304 | tf_op jit(solution)/shard_map/jit(_take)/gather | solution.py:95
  284.9 32.9 %gather_fusion.5 = f32[8192]{0:T(1024)S(1)} fusion(f32[1024]{0:T(1024)S(1)} %fusion.55, s32[8192]{0:T(1024)S(1)} %get-tuple-element.164), kind=kCustom, calls=%fused_computation.10.clone | custom fusion | bytes 98304 | tf_op jit(solution)/shard_map/jit(_take)/gather | solution.py:94
  317.9 32.9 %gather_fusion.10 = f32[8192]{0:T(1024)S(1)} fusion(f32[1024]{0:T(1024)S(1)} %fusion.55, s32[8192]{0:T(1024)S(1)} %get-tuple-element.161), kind=kCustom, calls=%fused_computation.13.clone | custom fusion | bytes 98304 | tf_op jit(solution)/shard_map/jit(_take)/gather | solution.py:95
  354.0 6.7 constant_dynamic-slice_fusion.3
  363.0 45.5 %gather_fusion.3 = f32[8192]{0:T(1024)S(1)} fusion(f32[32768]{0:T(1024)S(1)} %bitcast.106, s32[8192]{0:T(1024)S(1)} %get-tuple-element.156), kind=kCustom, calls=%fused_computation.2.clone | custom fusion | bytes 98304 | tf_op jit(solution)/shard_map/jit(_take)/gather | solution.py:93
  408.6 45.5 %gather_fusion = f32[8192]{0:T(1024)S(1)} fusion(f32[32768]{0:T(1024)S(1)} %bitcast.107, s32[8192]{0:T(1024)S(1)} %get-tuple-element.155), kind=kCustom, calls=%fused_computation.clone | custom fusion | bytes 98304 | tf_op jit(solution)/shard_map/jit(_take)/gather | solution.py:92
  454.8 9.4 psum.87
  464.2 32.9 %gather_fusion.9 = f32[8192]{0:T(1024)S(1)} fusion(f32[1024]{0:T(1024)S(1)} %fusion.55, s32[8192]{0:T(1024)S(1)} %get-tuple-element.162), kind=kCustom, calls=%fused_computation.12.clone | custom fusion | bytes 98304 | tf_op jit(solution)/shard_map/jit(_take)/gather | solution.py:94
  497.1 9.5 psum.88
  510.7 16.2 %psum.89 = f32[]{:T(128)} all-reduce(f32[]{:T(128)} %psum.88), channel_id=1, replica_groups=mesh['agent_0'=4,'agent_1'=4,'agent_2'=8,'grid'=2] {'agent_2'}, use_global_device_ids=true, to_apply=%region_16.19 | all-reduce | flops 1 | bytes 8 | tf_op jit(solution)/shard_map/psum | solution.py:40
  530.2 45.5 %gather_fusion.7 = f32[8192]{0:T(1024)S(1)} fusion(f32[32768]{0:T(1024)S(1)} %bitcast.108, s32[8192]{0:T(1024)S(1)} %get-tuple-element.154), kind=kCustom, calls=%fused_computation.4.clone | custom fusion | bytes 98304 | tf_op jit(solution)/shard_map/jit(_take)/gather | solution.py:93
  575.8 45.5 %gather_fusion.4 = f32[8192]{0:T(1024)S(1)} fusion(f32[32768]{0:T(1024)S(1)} %bitcast.109, s32[8192]{0:T(1024)S(1)} %get-tuple-element.153), kind=kCustom, calls=%fused_computation.3.clone | custom fusion | bytes 98304 | tf_op jit(solution)/shard_map/jit(_take)/gather | solution.py:92
  622.0 9.2 psum.90
  631.2 32.9 %gather_fusion.14 = f32[8192]{0:T(1024)S(1)} fusion(f32[1024]{0:T(1024)S(1)} %fusion.55, s32[8192]{0:T(1024)S(1)} %get-tuple-element.158), kind=kCustom, calls=%fused_computation.15.clone | custom fusion | bytes 98304 | tf_op jit(solution)/shard_map/jit(_take)/gather | solution.py:95
  664.1 9.0 psum.91
  677.2 16.0 %psum.92 = f32[]{:T(128)} all-reduce(f32[]{:T(128)} %psum.91), channel_id=1, replica_groups=mesh['agent_0'=4,'agent_1'=4,'agent_2'=8,'grid'=2] {'agent_2'}, use_global_device_ids=true, to_apply=%region_20.23 | all-reduce | flops 1 | bytes 8 | tf_op jit(solution)/shard_map/psum | solution.py:40
  696.6 45.5 %gather_fusion.11 = f32[8192]{0:T(1024)S(1)} fusion(f32[32768]{0:T(1024)S(1)} %bitcast.110, s32[8192]{0:T(1024)S(1)} %get-tuple-element.152), kind=kCustom, calls=%fused_computation.6.clone | custom fusion | bytes 98304 | tf_op jit(solution)/shard_map/jit(_take)/gather | solution.py:93
  742.1 45.5 %gather_fusion.8 = f32[8192]{0:T(1024)S(1)} fusion(f32[32768]{0:T(1024)S(1)} %bitcast.111, s32[8192]{0:T(1024)S(1)} %get-tuple-element.151), kind=kCustom, calls=%fused_computation.5.clone | custom fusion | bytes 98304 | tf_op jit(solution)/shard_map/jit(_take)/gather | solution.py:92
  788.3 9.4 psum.93
  797.7 32.9 %gather_fusion.13 = f32[8192]{0:T(1024)S(1)} fusion(f32[1024]{0:T(1024)S(1)} %fusion.55, s32[8192]{0:T(1024)S(1)} %get-tuple-element.157), kind=kCustom, calls=%fused_computation.14.clone | custom fusion | bytes 98304 | tf_op jit(solution)/shard_map/jit(_take)/gather | solution.py:94
  830.6 9.5 psum.94
  842.6 16.2 %psum.95 = f32[]{:T(128)} all-reduce(f32[]{:T(128)} %psum.94), channel_id=1, replica_groups=mesh['agent_0'=4,'agent_1'=4,'agent_2'=8,'grid'=2] {'agent_2'}, use_global_device_ids=true, to_apply=%region_24.27 | all-reduce | flops 1 | bytes 8 | tf_op jit(solution)/shard_map/psum | solution.py:40
  862.1 45.5 %gather_fusion.15 = f32[8192]{0:T(1024)S(1)} fusion(f32[32768]{0:T(1024)S(1)} %bitcast.112, s32[8192]{0:T(1024)S(1)} %get-tuple-element.159), kind=kCustom, calls=%fused_computation.8.clone | custom fusion | bytes 98304 | tf_op jit(solution)/shard_map/jit(_take)/gather | solution.py:93
  907.7 45.5 %gather_fusion.12 = f32[8192]{0:T(1024)S(1)} fusion(f32[32768]{0:T(1024)S(1)} %bitcast.113, s32[8192]{0:T(1024)S(1)} %get-tuple-element.160), kind=kCustom, calls=%fused_computation.7.clone | custom fusion | bytes 98304 | tf_op jit(solution)/shard_map/jit(_take)/gather | solution.py:92
  (230 shorter events, 137.2 us)
Async XLA Ops:
  10.0 18.9 %copy-start.5 = (f32[4,16]{1,0:T(4,128)S(1)}, f32[4,16]{1,0:T(4,128)}, u32[]{:S(2)}) copy-start(f32[4,16]{1,0:T(4,128)} %param.22) | copy-start | bytes 772
  10.0 19.0 %copy-start.6 = (f32[4,16]{1,0:T(4,128)S(1)}, f32[4,16]{1,0:T(4,128)}, u32[]{:S(2)}) copy-start(f32[4,16]{1,0:T(4,128)} %param.21) | copy-start | bytes 772
  10.1 19.2 %copy-start.7 = (f32[32]{0:T(128)S(1)}, f32[32]{0:T(128)}, u32[]{:S(2)}) copy-start(f32[32]{0:T(128)} %param.23) | copy-start | bytes 388
  13.5 26.4 %all-to-all-start = ((f32[128,1,128]{2,1,0:T(1,128)}), f32[128,1,128]{2,1,0:T(1,128)S(1)}, u32[]{:S(2)}, u32[]{:S(2)}) async-start(f32[128,1,128]{2,1,0:T(1,128)} %reshape.401), calls=%async_computation | async-start | bytes 131072 | tf_op jit(solution)/shard_map/all_to_all | solution.py:129
  28.8 325.1 %all-gather.2.cloned.1.call-start = ((), (), s32[]{:S(2)}) async-start(), calls=%async_computation.2 | async-start | bytes 8454144 | tf_op jit(solution)/shard_map/all_gather | solution.py:147
  41.6 103.1 %copy-start.2 = (f32[8192]{0:T(1024)S(1)}, f32[8192]{0:T(1024)}, u32[]{:S(2)}) copy-start(f32[8192]{0:T(1024)} %param.24) | copy-start | bytes 98308
  41.6 138.5 %copy-start.4 = (s32[4]{0:T(128)S(1)}, s32[4]{0:T(128)}, u32[]{:S(2)}) copy-start(s32[4]{0:T(128)} %param.27) | copy-start | bytes 52
  41.7 144.3 %copy-start = (s32[4,8192]{1,0:T(4,128)S(1)}, s32[4,8192]{1,0:T(4,128)}, u32[]{:S(2)}) copy-start(s32[4,8192]{1,0:T(4,128)} %param.25) | copy-start | bytes 393220
  41.7 144.4 %copy-start.1 = (s32[4,8192]{1,0:T(4,128)S(1)}, s32[4,8192]{1,0:T(4,128)}, u32[]{:S(2)}) copy-start(s32[4,8192]{1,0:T(4,128)} %param.26) | copy-start | bytes 393220
  140.3 78.8 %copy-start.3 = (f32[16,512]{1,0:T(8,128)}, f32[16,512]{1,0:T(8,128)S(1)}, u32[]{:S(2)}) copy-start(f32[16,512]{1,0:T(8,128)S(1)} %get-tuple-element.49) | copy-start | bytes 98308
Sparse Core Ops, SparseCore 0:
  144.9 117.9 all-gather.1
where the time goes:
time: 964 us; the launch traced here: 961 us
  local copies, waits for them, and re-layouts  692 us (72%)
  blocking collectives  143 us (15%)
  other arithmetic  65.1 us (7%)
  between operations  24.8 us (3%)
  starting transfers between devices  15.4 us (2%)
  matrix products  10.4 us (1%)
  waiting for transfers between devices  10.4 us (1%)
    gather x4, local copies, waits for them, and re-layouts, advance(): value_high = jnp.take(flattened, flat_index + 1)  182 us
    gather x4, local copies, waits for them, and re-layouts, advance(): value_low = jnp.take(flattened, flat_index)  182 us
    psum x12, blocking collectives, over_axes(): x = lax.psum(x, axis)  139 us
    gather x4, local copies, waits for them, and re-layouts, advance(): edge_high = jnp.take(points, bracket_row + 1)  131 us
    gather x4, local copies, waits for them, and re-layouts, advance(): edge_low = jnp.take(points, bracket_row)  131 us
    dynamic_update_slice x32, local copies, waits for them, and re-layouts, on_device(): values_now, policy = lax.map(one_state, (expected, growth, income))  22 us
    reduce_sum x16, other arithmetic, bellman(): chosen = jnp.sum(weight * points[None, :], axis=1) / totals  21.9 us
    add x16, other arithmetic, one_state(): return bellman(points, own_points * factor + earned, column)  20.7 us
  transfers between devices with their start and end apart: 2, of which 1 were waited for; matrix products, arithmetic and copies ran while one was open for 17% of the time, Pallas kernels for 0%

commit v1 on v0

v1 whole, which is shorter than its diff:
```python
import jax
import jax.numpy as jnp
from jax import lax
from jax.experimental import pallas as pl
from jax.experimental.pallas import tpu as pltpu
from jax.sharding import Mesh
from jax.sharding import PartitionSpec as P
MESH=pl.DeviceIdType.MESH
X,Y,ZC,G="agent_0","agent_1","agent_2","grid"
AGENT=(X,Y,ZC)
NK=16
f32=jnp.float32
i32=jnp.int32
LOG2E=1.4426950408889634
KT=500.0*LOG2E
SP=40.0/15
UN=32

def chip_id(a):
    return {X: a//32, Y: (a//8)%4, ZC: a%8}

def expect_kernel(vt_ref, tw_ref, coef_ref, const_ref, out_ref, send, recv, sem_s, sem_r):
    me=lax.axis_index(X)*32+lax.axis_index(Y)*8+lax.axis_index(ZC)
    bar=pltpu.get_barrier_semaphore()
    def sig(d,_):
        pl.semaphore_signal(bar,inc=1,device_id=chip_id(lax.rem(me+d,128)),device_id_type=MESH)
        return 0
    lax.fori_loop(1,128,sig,0)
    lane=lax.broadcasted_iota(jnp.int32,(8,128),1)
    sub=lax.broadcasted_iota(jnp.int32,(8,128),0)
    tw=tw_ref[...]
    tn=tw/jnp.sum(tw,axis=1,keepdims=True)
    blocks=[]
    for k in range(NK):
        b=None
        for y in range(4):
            col=(y*4+k//4)*128
            x=vt_ref[:,col:col+128]
            s=(y*32-(k%4)*32)%128
            if s: x=pltpu.roll(x,s,1)
            b=x if b is None else jnp.where(lane//32==y,x,b)
        blocks.append(b)
    vk=jnp.concatenate(blocks,axis=0)
    bl=lax.dot_general(vk,tn,(((1,),(1,)),((),())),precision=lax.Precision.HIGHEST,preferred_element_type=f32)
    zl=lane//32
    cf=jnp.where(zl==0,coef_ref[0],jnp.where(zl==1,coef_ref[1],jnp.where(zl==2,coef_ref[2],coef_ref[3])))
    cs=jnp.where(zl==0,const_ref[0],jnp.where(zl==1,const_ref[1],jnp.where(zl==2,const_ref[2],const_ref[3])))
    masks=[(lane//16-sub)%8==d for d in range(8)]
    for j in range(NK):
        fc=jnp.clip(cf*(40.0*j/15)+cs,0.0,40.0)
        acc=None
        for k in range(NK):
            h=jnp.maximum(0.0,1.0-jnp.abs(fc-(40.0*k/15))/SP)
            t=h*bl[k*8:k*8+8,:]
            acc=t if acc is None else acc+t
        o=acc
        for d in range(1,8):
            r=pltpu.roll(pltpu.roll(acc,(8-d)%8,0),16*d,1)
            o=jnp.where(masks[d],r,o)
        for g in range(8):
            send[j*8+g]=o[g:g+1,:]
    pl.semaphore_wait(bar,127)
    def row_of(a):
        return (a%32)//2*8+(a//32)*2+a%2
    def cp(d):
        a=lax.rem(me+d,128)
        return pltpu.make_async_remote_copy(src_ref=send.at[row_of(a)],dst_ref=recv.at[me],send_sem=sem_s,recv_sem=sem_r,device_id=chip_id(a),device_id_type=MESH)
    def go(d,_):
        cp(d).start()
        return 0
    lax.fori_loop(1,128,go,0)
    recv[me]=send[row_of(me)]
    pltpu.make_async_copy(recv.at[pl.ds(0,127)],recv.at[pl.ds(0,127)],sem_r).wait()
    for A in range(16):
        out_ref[A*8:A*8+8,:]=jnp.concatenate([recv[A*8+s] for s in range(8)],axis=0)
    pltpu.make_async_copy(send.at[pl.ds(0,127)],send.at[pl.ds(0,127)],sem_s).wait()

def expect(vt,tw,coef,const):
    vm=pl.BlockSpec(memory_space=pltpu.VMEM); sm=pl.BlockSpec(memory_space=pltpu.SMEM)
    return pl.pallas_call(expect_kernel,out_shape=jax.ShapeDtypeStruct((128,128),f32),
        in_specs=[vm,vm,sm,sm],out_specs=vm,
        scratch_shapes=[pltpu.VMEM((128,1,128),f32),pltpu.VMEM((128,1,128),f32),pltpu.SemaphoreType.DMA,pltpu.SemaphoreType.DMA],
        compiler_params=pltpu.CompilerParams(collective_id=0,has_side_effects=True),name="expect")(vt,tw,coef,const)


def hat(x,k):
    return jnp.maximum(0.0,1.0-jnp.abs(x-40.0*k/15)/SP)

def rdma(src,dst,ss,rs,**dev):
    return pltpu.make_async_remote_copy(src_ref=src,dst_ref=dst,send_sem=ss,recv_sem=rs,device_id=dev_ids(dev),device_id_type=MESH)
def dev_ids(dev):
    return {dict(x=X,y=Y,z=ZC,g=G)[k]:v for k,v in dev.items()}
def got(ref,sem):
    pltpu.make_async_copy(ref,ref,sem).wait()

def life(r_ref, hold_ref, shock_ref, brack_ref, int_ref, wage_ref, eff_ref, agg_ref,
         v_ref, p_ref, h_ref, cap_ref,
         pt,kpt,sc,rs,vb,pb,
         pxa,pxb,y0,z0,yb,lk,tt,oh,res,ri,li,pbk,inv,hp,hr,pay1,in1,pay2,in2,
         sx,rx,sy0,ry0,sz0,rz0,szt,rzt,sya,rya,syb,ryb,sh,rh,s1,r1,s2,r2):
    px=(pxa,pxb)
    x=lax.axis_index(X); y=lax.axis_index(Y); zc=lax.axis_index(ZC); g=lax.axis_index(G)
    bar=pltpu.get_barrier_semaphore()
    me_p=x*4+y
    me_l=zc*2+g
    def plane(d):
        o=lax.rem(me_p+d,16)
        return {X:o//4,Y:lax.rem(o,4)}
    def line(d):
        o=lax.rem(me_l+d,16)
        return {ZC:o//2,G:lax.rem(o,2)}
    def sig(d,_):
        pl.semaphore_signal(bar,inc=1,device_id=plane(d),device_id_type=MESH)
        pl.semaphore_signal(bar,inc=1,device_id=line(d),device_id_type=MESH)
        return 0
    lax.fori_loop(1,16,sig,0)

    def pts(A,_):
        for n in range(8):
            t=A*8+n
            j=(64*A+n+8*lax.broadcasted_iota(i32,(8,128),0)).astype(f32)
            fr=j/1023.0
            p=40.0*fr*fr
            o=pl.multiple_of(t*8,8)
            pt[pl.ds(o,8),:]=p
            kpt[pl.ds(o,8),:]=p*KT+0.1*KT
        return 0
    lax.fori_loop(0,16,pts,0)
    rs[...]=r_ref[...]*(48.0*LOG2E)
    k=y*4+zc//2
    eh=lax.rem(zc,2)
    growth=1.0+int_ref[x,k]
    wage=wage_ref[x,k]
    def state(e,_):
        inc=wage*eff_ref[eh*16+e]
        W=[];KW=[]
        for v in range(4):
            i=(lax.broadcasted_iota(i32,(8,128),1)+(128*v+512*g)).astype(f32)
            fr=i/1023.0
            w=(40.0*fr*fr)*growth+inc
            W.append(w);KW.append(w*KT)
        def p1(c,M):
            M=list(M)
            for u in range(UN):
                off=pl.multiple_of((c*UN+u)*8,8)
                P=pt[pl.ds(off,8),:]; KP=kpt[pl.ds(off,8),:]
                Rr=rs[pl.ds(pl.multiple_of((c*(UN//8)+u//8)*8,8),8),:]
                B=jnp.take_along_axis(Rr,jnp.full((8,128),(u%8)*16+e,i32),axis=1,mode="promise_in_bounds")
                D=B-KP
                for v in range(4):
                    cl=jnp.maximum(W[v]-P,0.1)
                    S=jnp.log(cl)*(50.0*LOG2E)+jnp.minimum(KW[v]+D,B)
                    sc[pl.ds(off,8),128*v:128*v+128]=S
                    M[v]=jnp.maximum(M[v],S)
            return tuple(M)
        M=lax.fori_loop(0,128//UN,p1,tuple(jnp.full((8,128),-1e30,f32) for _ in range(4)))
        def p2(c,acc):
            acc=list(acc)
            for u in range(UN):
                off=pl.multiple_of((c*UN+u)*8,8)
                P=pt[pl.ds(off,8),:]
                for v in range(4):
                    q=jnp.exp2(sc[pl.ds(off,8),128*v:128*v+128]-M[v])
                    acc[v]=acc[v]+q
                    acc[4+v]=acc[4+v]+P*q
            return tuple(acc)
        acc=lax.fori_loop(0,128//UN,p2,tuple(jnp.zeros((8,128),f32) for _ in range(8)))
        for v in range(4):
            m=jnp.max(M[v],axis=0,keepdims=True)
            s=jnp.exp2(M[v]-m)
            tot=jnp.sum(acc[v]*s,axis=0,keepdims=True)
            q=jnp.sum(acc[4+v]*s,axis=0,keepdims=True)
            vb[e,:,128*v:128*v+128]=jnp.broadcast_to((0.02/LOG2E)*m+0.02*jnp.log(tot),(8,128))
            pb[e,:,128*v:128*v+128]=jnp.broadcast_to(q/tot,(8,128))
        return 0
    def bell(a,b):
        lax.fori_loop(a,b,state,0)
    def finish(c):
        v_ref[c*8:c*8+8,:]=jnp.concatenate([vb[c*8+s,0:1,:] for s in range(8)],axis=0)
        p=jnp.concatenate([pb[c*8+s,0:1,:] for s in range(8)],axis=0)
        p_ref[c*8:c*8+8,:]=p
        px[c][x]=p

    def send_x(c):
        def go(d,_):
            rdma(px[c].at[x],px[c].at[x],sx.at[c],rx.at[c],x=lax.rem(x+d,4)).start()
            return 0
        lax.fori_loop(1,4,go,0)
    def send_y0(c,w):
        got(px[c].at[pl.ds(0,3)],rx.at[c])
        y0[c,y]=px[c][agg_ref[0]]*w
        def go(d,_):
            rdma(y0.at[c,y],y0.at[c,y],sy0.at[c],ry0.at[c],y=lax.rem(y+d,4)).start()
            return 0
        lax.fori_loop(1,4,go,0)
    def send_z0(c):
        got(y0.at[c,pl.ds(0,3)],ry0.at[c])
        z0[c,zc]=(y0[c,0]+y0[c,1])+(y0[c,2]+y0[c,3])
        def go(d,_):
            rdma(z0.at[c,zc],z0.at[c,zc],sz0.at[c],rz0.at[c],z=lax.rem(zc+d,8)).start()
            return 0
        lax.fori_loop(1,8,go,0)
    def table0(c):
        got(z0.at[c,pl.ds(0,7)],rz0.at[c])
        for h in range(2):
            lk[h*16+c*8:h*16+c*8+8,:]=(z0[c,h]+z0[c,2+h])+(z0[c,4+h]+z0[c,6+h])
    def send_slot(t):
        for c in range(2):
            yb[t-1,y,zc,c]=px[c][agg_ref[t]]
        def go(d,_):
            rdma(yb.at[t-1,y,zc],yb.at[t-1,y,zc],szt.at[t-1],rzt.at[t-1],z=lax.rem(zc+d,8)).start()
            return 0
        lax.fori_loop(1,8,go,0)
    up=lax.rem(y+1,4); down=lax.rem(y+3,4)
    def slot_a(t):
        got(yb.at[t-1,0,pl.ds(0,7)],rzt.at[t-1])
        for n,d in ((0,up),(1,down)):
            rdma(yb.at[t-1,y],yb.at[t-1,y],sya.at[t-1,n],rya.at[t-1,n],y=d).start()
    def slot_b(t):
        got(yb.at[t-1,0],rya.at[t-1,0])
        rdma(yb.at[t-1,down,pl.ds(0,4)],yb.at[t-1,down,pl.ds(0,4)],syb.at[t-1,0],ryb.at[t-1,0],y=up).start()
        got(yb.at[t-1,0],rya.at[t-1,1])
        rdma(yb.at[t-1,up,pl.ds(4,4)],yb.at[t-1,up,pl.ds(4,4)],syb.at[t-1,1],ryb.at[t-1,1],y=down).start()
    def slot_done(t):
        got(yb.at[t-1,0,pl.ds(0,4)],ryb.at[t-1,0])
        got(yb.at[t-1,0,pl.ds(0,4)],ryb.at[t-1,1])
    def table(t,cap):
        hs=[hat(cap,q) for q in range(16)]
        for h in range(2):
            for c in range(2):
                for v in range(4):
                    acc=None
                    for q in range(16):
                        w=hs[q]*yb[t-1,q//4,2*(q%4)+h,c,:,128*v:128*v+128]
                        acc=w if acc is None else acc+w
                    lk[h*16+c*8:h*16+c*8+8,128*v:128*v+128]=acc

    def sum_a(t,row):
        pay1[t]=row
        in1[t,me_l]=row
        def go(d,_):
            dv=line(d)
            pltpu.make_async_remote_copy(src_ref=pay1.at[t],dst_ref=in1.at[t,me_l],send_sem=s1.at[t],recv_sem=r1.at[t],device_id=dv,device_id_type=MESH).start()
            return 0
        lax.fori_loop(1,16,go,0)
    def total(buf,t):
        rows=[buf[t,n] for n in range(16)]
        while len(rows)>1:
            rows=[rows[2*n]+rows[2*n+1] for n in range(len(rows)//2)]
        return rows[0]
    def sum_b(t):
        got(in1.at[t,pl.ds(0,15)],r1.at[t])
        row=total(in1,t)
        pay2[t]=row
        in2[t,me_p]=row
        def go(d,_):
            dv=plane(d)
            pltpu.make_async_remote_copy(src_ref=pay2.at[t],dst_ref=in2.at[t,me_p],send_sem=s2.at[t],recv_sem=r2.at[t],device_id=dv,device_id_type=MESH).start()
            return 0
        lax.fori_loop(1,16,go,0)
    def sum_c(t):
        got(in2.at[t,pl.ds(0,15)],r2.at[t])
        cap=jnp.sum(total(in2,t))/1048576.0
        cap_ref[t]=cap
        return cap

    def index(n,_):
        cols=pl.ds(pl.multiple_of(n*1024,1024),1024)
        b=brack_ref[:,cols]; s=shock_ref[:,cols]
        edge=b==511
        own=(b//512)==g
        r=((b//128)%4)*32+s
        ri[:,cols]=jnp.where(own,r,jnp.where(jnp.logical_and(edge,g==1),s,-1))
        li[:,cols]=jnp.where(jnp.logical_and(edge,g==1),0,b%128)
        fa=b.astype(f32)/1023.0; fb=(b+1).astype(f32)/1023.0
        lo=40.0*fa*fa; hi=40.0*fb*fb
        pbk[:,cols]=lo
        inv[:,cols]=1.0/(hi-lo)
        return 0
    lane=lax.broadcasted_iota(i32,(32,128),1)
    iota=lax.broadcasted_iota(i32,(128,128),0)
    gf=g.astype(f32)
    def evolve(t):
        ls=[lk[:,128*v:128*v+128] for v in range(4)]
        ro=[pltpu.roll(q,127,1) for q in ls]
        ds=[]
        for v in range(4):
            nx=ro[v+1] if v<3 else ro[v]
            ds.append(jnp.where(lane==127,nx,ro[v])-ls[v])
        for o,q in ((0,ls),(128,ds)):
            m=jnp.concatenate(q,axis=0).T
            hi=m.astype(jnp.bfloat16)
            tt[o:o+128,0:128]=hi
            tt[o:o+128,128:256]=(m-hi.astype(f32)).astype(jnp.bfloat16)
        def grp(n,acc):
            base=n*1024
            for q in range(8):
                cols=pl.ds(pl.multiple_of(base+q*128,128),128)
                o=jnp.where(jnp.broadcast_to(ri[t:t+1,cols],(128,128))==iota,1.0,0.0).astype(jnp.bfloat16)
                oh[0:128,q*128:q*128+128]=o
                oh[128:256,q*128:q*128+128]=o
            res[...]=jnp.dot(tt[...],oh[...],preferred_element_type=f32)
            r8=pl.ds(pl.multiple_of(n*8,8),8)
            h=hold_ref[r8,:] if t==0 else hp[t-1,r8,:]+hr[t-1,r8,:]
            rows=[]
            for q in range(8):
                cols=pl.ds(pl.multiple_of(base+q*128,128),128)
                m=jnp.broadcast_to(li[t:t+1,cols],(128,128))==iota
                sl=jnp.sum(jnp.where(m,res[0:128,q*128:q*128+128],0.0),axis=0,keepdims=True)
                sd=jnp.sum(jnp.where(m,res[128:256,q*128:q*128+128],0.0),axis=0,keepdims=True)
                f=jnp.clip((h[q:q+1,:]-pbk[t:t+1,cols])*inv[t:t+1,cols],0.0,1.0)
                edge=brack_ref[t:t+1,cols]==511
                wl=jnp.where(edge,gf*f+(1.0-gf)*(1.0-f),1.0)
                wd=jnp.where(edge,0.0,f)
                rows.append(wl*sl+wd*sd)
            hn=jnp.concatenate(rows,axis=0)
            hp[t,r8,:]=hn
            return acc+hn
        acc=lax.fori_loop(0,8,grp,jnp.zeros((8,128),f32))
        rdma(hp.at[t],hr.at[t],sh.at[t],rh.at[t],g=1-g).start()
        return jnp.sum(acc,axis=0,keepdims=True)

    lax.fori_loop(0,8,index,0)
    h0=jnp.zeros((8,128),f32)
    for n in range(4):
        h0=h0+hold_ref[pl.ds(pl.multiple_of(g*32+n*8,8),8),:]
    pl.semaphore_wait(bar,30)
    sum_a(0,jnp.sum(h0,axis=0,keepdims=True))
    bell(0,4)
    sum_b(0)
    bell(4,8)
    finish(0)
    send_x(0)
    cap=sum_c(0)
    kf=k.astype(f32)
    w0=jnp.maximum(0.0,1.0-jnp.abs(cap-40.0*kf/15)/SP)
    bell(8,10)
    send_y0(0,w0)
    bell(10,12)
    send_z0(0)
    bell(12,16)
    finish(1)
    send_x(1)
    send_y0(1,w0)
    send_z0(1)
    for t in range(1,4):
        send_slot(t)
    table0(0)
    table0(1)
    for t in range(4):
        if t:
            slot_done(t)
            table(t,cap)
            got(hr.at[t-1],rh.at[t-1])
        row=evolve(t)
        if t<3:
            sum_a(t+1,row)
            if t==0:
                slot_a(1)
            sum_b(t+1)
            slot_b(t+1)
            if t<2:
                slot_a(t+2)
            cap=sum_c(t+1)
    got(hr.at[3],rh.at[3])
    h_ref[...]=hp[3]+hr[3]
    for c in range(2):
        got(px[c].at[pl.ds(0,3)],sx.at[c])
        got(y0.at[c,pl.ds(0,3)],sy0.at[c])
        got(z0.at[c,pl.ds(0,7)],sz0.at[c])
    for t in range(3):
        got(yb.at[t,0,pl.ds(0,7)],szt.at[t])
        for n in range(2):
            got(yb.at[t,0],sya.at[t,n])
            got(yb.at[t,0,pl.ds(0,4)],syb.at[t,n])
    for t in range(4):
        got(hp.at[t],sh.at[t])
        got(in1.at[t,pl.ds(0,15)],s1.at[t])
        got(in2.at[t,pl.ds(0,15)],s2.at[t])

def life_call(r,hold,shock,brack,interest,wage,eff,agg):
    vm=pl.BlockSpec(memory_space=pltpu.VMEM); sm=pl.BlockSpec(memory_space=pltpu.SMEM)
    V=lambda *s: pltpu.VMEM(s,f32)
    S=lambda *s: pltpu.SemaphoreType.DMA(s)
    return pl.pallas_call(life,
        out_shape=[jax.ShapeDtypeStruct((16,512),f32),jax.ShapeDtypeStruct((16,512),f32),jax.ShapeDtypeStruct((64,128),f32),jax.ShapeDtypeStruct((4,),f32)],
        in_specs=[vm]*4+[sm]*4,out_specs=[vm,vm,vm,sm],
        scratch_shapes=[V(1024,128),V(1024,128),V(1024,512),V(128,128),V(16,8,512),V(16,8,512),
            V(4,8,512),V(4,8,512),V(2,4,8,512),V(2,8,8,512),V(3,4,8,2,8,512),V(32,512),pltpu.VMEM((256,256),jnp.bfloat16),pltpu.VMEM((256,1024),jnp.bfloat16),V(256,1024),
            pltpu.VMEM((4,8192),i32),pltpu.VMEM((4,8192),i32),V(4,8192),V(4,8192),V(4,64,128),V(4,64,128),V(4,1,128),V(4,16,1,128),V(4,1,128),V(4,16,1,128),
            S(2),S(2),S(2),S(2),S(2),S(2),S(3),S(3),S(3,2),S(3,2),S(3,2),S(3,2),S(4),S(4),S(4),S(4),S(4),S(4)],
        compiler_params=pltpu.CompilerParams(collective_id=1,has_side_effects=True,vmem_limit_bytes=40*1024*1024),name="life")(r,hold,shock,brack,interest,wage,eff,agg)


def on_device(value_prior,trans_weight,coefficient,constant,interest,wage_level,efficiency,holdings,shocks,brackets,aggregate):
    arrived=expect(value_prior.T,trans_weight,coefficient,constant)
    values_now,policy,final,capital=life_call(arrived,holdings.reshape(64,128),shocks,brackets,interest,wage_level,efficiency,aggregate)
    return values_now,policy,final.reshape(8192),capital


def solution(mesh):
    finer=Mesh(mesh.devices.reshape(4,4,8,mesh.shape["grid"]),(X,Y,ZC,G))
    in_specs=(P(None,AGENT),P(),P(),P(),P(),P(),P(),P(AGENT),P(None,AGENT),P(None,AGENT),P())
    out_specs=(P(AGENT,G),P(AGENT,G),P(AGENT),P())
    return jax.shard_map(on_device,mesh=finer,in_specs=in_specs,out_specs=out_specs,check_vma=False)
```

time: 964 us -> 123 us (0.13)
  the two profiles are of different devices: /device:TPU:8 before, /device:TPU:1 now
where the time goes in v1:
time: 123 us
  Pallas kernels  118 us (96%)
  local copies, waits for them, and re-layouts  4.12 us (3%)
    pallas_call x1, Pallas kernels, life_call(): pl.pallas_call(life, out_shape=[jax.ShapeDtypeStruct((16, 512), f32), jax...  95.4 us
    pallas_call x1, Pallas kernels, expect(): pl.pallas_call(expect_kernel, out_shape=jax.ShapeDtypeStruct((128, 128),...  22.6 us
    unnamed x20, local copies, waits for them, and re-layouts  4.12 us

profile of v1, /device:TPU:1, one launch (start us, length us, event | category | flops | bytes accessed | tf_op | source)
XLA Modules:
  0.0 122.8 jit_solution(4472223379094475378)
XLA Ops:
  0.6 0.0 copy-start.1
  0.6 0.0 copy-start.3
  0.7 0.0 copy-start.4
  0.7 0.0 copy-start.5
  0.7 0.0 copy-start.6
  0.7 0.0 copy-start.7
  0.7 22.6 %expect.1.r_ref = f32[128,128]{1,0:T(8,128)} custom-call(f32[8,2048]{1,0:T(8,128)} %bitcast.5, f32[128,128]{1,0:T(8,128)} %tw_ref.1, f32[4]{0:T(128)} %coef_ref.1, f32[4]{0:T(128)} %const_ref.1), custom_call_target="tpu_custom_call" | custom-call | tf_op jit(solution)/shard_map/expect/pallas_call | solution.py:80
  23.3 0.0 copy-done.1
  23.3 0.0 copy-done.3
  23.3 0.0 copy-done.4
  23.3 0.0 copy-done.5
  23.3 0.0 copy-done.6
  23.3 0.0 copy-done.7
  23.3 0.0 copy-start
  23.4 0.8 copy-done
  24.2 0.0 copy-start.2
  24.2 0.9 copy-done.2
  25.1 95.4 %life.1 = (f32[16,512]{1,0:T(8,128)S(1)}, f32[16,512]{1,0:T(8,128)S(1)}, f32[64,128]{1,0:T(8,128)S(1)}, f32[4]{0:T(128)S(1)}) custom-call(f32[128,128]{1,0:T(8,128)S(1)} %copy-done, f32[64,128]{1,0:T(8,128)S(1)} %bitcast.3, s32[4,8192]{1,0:T(4,128)S(1)} %copy-done.1, s32[4,8192]{1,0:T(4,128)S(1)} %copy-done.2, f32[4,16]{1,0:T(4,128)S(1)} %copy-done.4, ...), custom_call_target="tpu_custom_call" | custom-call | tf_op jit(solution)/shard_map/life/pallas_call | solution.py:385
  120.5 0.6 copy.19
  121.1 0.6 copy.20
  121.7 0.6 copy.21
  122.3 0.5 copy.22
Async XLA Ops:
  0.6 22.7 %copy-start.1 = (s32[4,8192]{1,0:T(4,128)S(1)}, s32[4,8192]{1,0:T(4,128)}, u32[]{:S(2)}) copy-start(s32[4,8192]{1,0:T(4,128)} %shock_ref.1) | copy-start | bytes 393220
  0.6 22.7 %copy-start.3 = (f32[8192]{0:T(1024)S(1)}, f32[8192]{0:T(1024)}, u32[]{:S(2)}) copy-start(f32[8192]{0:T(1024)} %param.18) | copy-start | bytes 98308
  0.7 22.7 %copy-start.4 = (f32[4,16]{1,0:T(4,128)S(1)}, f32[4,16]{1,0:T(4,128)}, u32[]{:S(2)}) copy-start(f32[4,16]{1,0:T(4,128)} %int_ref.1) | copy-start | bytes 772
  0.7 22.7 %copy-start.5 = (f32[4,16]{1,0:T(4,128)S(1)}, f32[4,16]{1,0:T(4,128)}, u32[]{:S(2)}) copy-start(f32[4,16]{1,0:T(4,128)} %wage_ref.1) | copy-start | bytes 772
  0.7 22.7 %copy-start.6 = (f32[32]{0:T(128)S(1)}, f32[32]{0:T(128)}, u32[]{:S(2)}) copy-start(f32[32]{0:T(128)} %eff_ref.1) | copy-start | bytes 388
  0.7 22.7 %copy-start.7 = (s32[4]{0:T(128)S(1)}, s32[4]{0:T(128)}, u32[]{:S(2)}) copy-start(s32[4]{0:T(128)} %agg_ref.1) | copy-start | bytes 52
  23.3 0.8 copy-start
  24.2 0.9 copy-start.2

commit v2 on v1

v2 whole, which is shorter than its diff:
```python
import jax
import jax.numpy as jnp
from jax import lax
from jax.experimental import pallas as pl
from jax.experimental.pallas import tpu as pltpu
from jax.sharding import Mesh
from jax.sharding import PartitionSpec as P
MESH=pl.DeviceIdType.MESH
X,Y,ZC,G="agent_0","agent_1","agent_2","grid"
AGENT=(X,Y,ZC)
f32=jnp.float32
i32=jnp.int32
LOG2E=1.4426950408889634
KT=500.0*LOG2E
SP=40.0/15
UN=32

def hat(x,k):
    return jnp.maximum(0.0,1.0-jnp.abs(x-40.0*k/15)/SP)

def rdma(src,dst,ss,rs,**dev):
    return pltpu.make_async_remote_copy(src_ref=src,dst_ref=dst,send_sem=ss,recv_sem=rs,device_id=dev_ids(dev),device_id_type=MESH)
def dev_ids(dev):
    return {dict(x=X,y=Y,z=ZC,g=G)[k]:v for k,v in dev.items()}
def got(ref,sem):
    pltpu.make_async_copy(ref,ref,sem).wait()


CH=((0,8),(8,4),(12,4))

def life(vt_hbm, tw_hbm, hold_hbm, shock_hbm, brack_hbm, coef_ref, const_ref, int_ref, wage_ref, eff_ref, agg_ref,
         v_ref, p_ref, h_ref, cap_ref,
         vt_ref,tw_ref,hold_ref,shock_ref,brack_ref,send,mid,recv,
         pt,kpt,sc,rs,vb,pb,
         pxa,pxb,pxc,y0a,y0b,y0c,z0a,z0b,z0c,yba,ybb,lk,tt,oh,resa,resb,ri,li,own,pbk,inv,fr_s,hp,hr,pay1,in1,pay2,in2,wt,cl,ctot,
         sin,sa1,ra1,sa2,ra2,sx,rx,sy0,ry0,sz0,rz0,szt,rzt,sya,rya,syb,ryb,sh,rh,s1,r1,s2,r2):
    px=(pxa,pxb,pxc); y0=(y0a,y0b,y0c); z0=(z0a,z0b,z0c); yb=(yba,ybb); res=(resa,resb)
    x=lax.axis_index(X); y=lax.axis_index(Y); zc=lax.axis_index(ZC); g=lax.axis_index(G)
    inputs=[pltpu.make_async_copy(a,b,sin.at[n]) for n,(a,b) in enumerate(((vt_hbm,vt_ref),(tw_hbm,tw_ref),(hold_hbm,hold_ref),(shock_hbm,shock_ref),(brack_hbm,brack_ref)))]
    for c in inputs:
        c.start()
    bar=pltpu.get_barrier_semaphore()
    me_p=x*4+y
    me_l=zc*2+g
    def plane(d):
        o=lax.rem(me_p+d,16)
        return {X:o//4,Y:lax.rem(o,4)}
    def line(d):
        o=lax.rem(me_l+d,16)
        return {ZC:o//2,G:lax.rem(o,2)}
    def sig(d,_):
        pl.semaphore_signal(bar,inc=1,device_id=plane(d),device_id_type=MESH)
        pl.semaphore_signal(bar,inc=1,device_id=line(d),device_id_type=MESH)
        return 0
    lax.fori_loop(1,16,sig,0)

    lane8=lax.broadcasted_iota(i32,(8,128),1)
    sub8=lax.broadcasted_iota(i32,(8,128),0)
    def expect():
        inputs[0].wait(); inputs[1].wait()
        tw=tw_ref[...]
        tn=tw/jnp.sum(tw,axis=1,keepdims=True)
        blocks=[]
        for k in range(16):
            b=None
            for q in range(4):
                col=(q*4+k//4)*128
                w=vt_ref[:,col:col+128]
                d=(q*32-(k%4)*32)%128
                if d: w=pltpu.roll(w,d,1)
                b=w if b is None else jnp.where(lane8//32==q,w,b)
            blocks.append(b)
        vk=jnp.concatenate(blocks,axis=0)
        bl=lax.dot_general(vk,tn,(((1,),(1,)),((),())),precision=lax.Precision.HIGHEST,preferred_element_type=f32)
        zl=lane8//32
        def per_zone(r):
            return jnp.where(zl==0,r[0],jnp.where(zl==1,r[1],jnp.where(zl==2,r[2],r[3])))
        cf=per_zone(coef_ref); cs=per_zone(const_ref)
        masks=[(lane8//16-sub8)%8==d for d in range(8)]
        for j in range(16):
            fc=jnp.clip(cf*(40.0*j/15)+cs,0.0,40.0)
            acc=None
            for k in range(16):
                w=hat(fc,k)*bl[k*8:k*8+8,:]
                acc=w if acc is None else acc+w
            o=acc
            for d in range(1,8):
                o=jnp.where(masks[d],pltpu.roll(pltpu.roll(acc,8-d,0),16*d,1),o)
            for q in range(8):
                send[(j%4)*2+q%2,(q//2)*4+j//4]=o[q:q+1,:]
    def expect_a():
        def go(d,_):
            o=lax.rem(zc+d,8)
            rdma(send.at[o],mid.at[zc],sa1,ra1,z=o).start()
            return 0
        lax.fori_loop(1,8,go,0)
        mid[zc]=send[zc]
    def expect_b():
        got(mid.at[pl.ds(0,7)],ra1)
        def go(d,_):
            o=lax.rem(me_p+d,16)
            rdma(mid.at[:,o],recv.at[me_p],sa2,ra2,x=o//4,y=lax.rem(o,4)).start()
            return 0
        lax.fori_loop(1,16,go,0)
        recv[me_p]=mid[:,me_p]
    def expect_c():
        got(recv.at[pl.ds(0,15)],ra2)
        for q in range(16):
            rs[q*8:q*8+8,:]=jnp.concatenate([recv[q,n] for n in range(8)],axis=0)*(48.0*LOG2E)

    def pts(A,_):
        for n in range(8):
            t=A*8+n
            j=(64*A+n+8*sub8).astype(f32)
            fr=j/1023.0
            p=40.0*fr*fr
            o=pl.multiple_of(t*8,8)
            pt[pl.ds(o,8),:]=p
            kpt[pl.ds(o,8),:]=p*KT+0.1*KT
        return 0
    k=y*4+zc//2
    eh=lax.rem(zc,2)
    growth=1.0+int_ref[x,k]
    wage=wage_ref[x,k]
    def state(e,_):
        inc=wage*eff_ref[eh*16+e]
        W=[];KW=[]
        for v in range(4):
            i=(lax.broadcasted_iota(i32,(8,128),1)+(128*v+512*g)).astype(f32)
            fr=i/1023.0
            w=(40.0*fr*fr)*growth+inc
            W.append(w);KW.append(w*KT)
        def p1(c,M):
            M=list(M)
            for u in range(UN):
                off=pl.multiple_of((c*UN+u)*8,8)
                P=pt[pl.ds(off,8),:]; KP=kpt[pl.ds(off,8),:]
                Rr=rs[pl.ds(pl.multiple_of((c*(UN//8)+u//8)*8,8),8),:]
                B=jnp.take_along_axis(Rr,jnp.full((8,128),(u%8)*16+e,i32),axis=1,mode="promise_in_bounds")
                D=B-KP
                for v in range(4):
                    cl=jnp.maximum(W[v]-P,0.1)
                    S=jnp.log(cl)*(50.0*LOG2E)+jnp.minimum(KW[v]+D,B)
                    sc[pl.ds(off,8),128*v:128*v+128]=S
                    M[v]=jnp.maximum(M[v],S)
            return tuple(M)
        M=lax.fori_loop(0,128//UN,p1,tuple(jnp.full((8,128),-1e30,f32) for _ in range(4)))
        def p2(c,acc):
            acc=list(acc)
            for u in range(UN):
                off=pl.multiple_of((c*UN+u)*8,8)
                P=pt[pl.ds(off,8),:]
                for v in range(4):
                    q=jnp.exp2(sc[pl.ds(off,8),128*v:128*v+128]-M[v])
                    acc[v]=acc[v]+q
                    acc[4+v]=acc[4+v]+P*q
            return tuple(acc)
        acc=lax.fori_loop(0,128//UN,p2,tuple(jnp.zeros((8,128),f32) for _ in range(8)))
        for v in range(4):
            m=jnp.max(M[v],axis=0,keepdims=True)
            s=jnp.exp2(M[v]-m)
            tot=jnp.sum(acc[v]*s,axis=0,keepdims=True)
            q=jnp.sum(acc[4+v]*s,axis=0,keepdims=True)
            vb[e,:,128*v:128*v+128]=jnp.broadcast_to((0.02/LOG2E)*m+0.02*jnp.log(tot),(8,128))
            pb[e,:,128*v:128*v+128]=jnp.broadcast_to(q/tot,(8,128))
        return 0
    def bell(a,b):
        lax.fori_loop(a,b,state,0)
    def finish(c):
        a,n=CH[c]
        v_ref[a:a+n,:]=jnp.concatenate([vb[a+q,0:1,:] for q in range(n)],axis=0)
        p=jnp.concatenate([pb[a+q,0:1,:] for q in range(n)],axis=0)
        p_ref[a:a+n,:]=p
        px[c][x]=p

    def send_x(c):
        def go(d,_):
            rdma(px[c].at[x],px[c].at[x],sx.at[c],rx.at[c],x=lax.rem(x+d,4)).start()
            return 0
        lax.fori_loop(1,4,go,0)
    def send_y0(c,w):
        got(px[c].at[pl.ds(0,3)],rx.at[c])
        y0[c][y]=px[c][agg_ref[0]]*w
        def go(d,_):
            rdma(y0[c].at[y],y0[c].at[y],sy0.at[c],ry0.at[c],y=lax.rem(y+d,4)).start()
            return 0
        lax.fori_loop(1,4,go,0)
    def send_z0(c):
        got(y0[c].at[pl.ds(0,3)],ry0.at[c])
        b=y0[c]
        z0[c][zc]=(b[0]+b[1])+(b[2]+b[3])
        def go(d,_):
            rdma(z0[c].at[zc],z0[c].at[zc],sz0.at[c],rz0.at[c],z=lax.rem(zc+d,8)).start()
            return 0
        lax.fori_loop(1,8,go,0)
    def table0(c):
        got(z0[c].at[pl.ds(0,7)],rz0.at[c])
        a,n=CH[c]
        b=z0[c]
        for h in range(2):
            lk[h*16+a:h*16+a+n,:]=(b[h]+b[2+h])+(b[4+h]+b[6+h])
    def send_slot(t,half):
        b=yb[half]
        if half==0:
            b[t-1,y,zc]=px[0][agg_ref[t]]
        else:
            b[t-1,y,zc,0:4]=px[1][agg_ref[t]]
            b[t-1,y,zc,4:8]=px[2][agg_ref[t]]
        def go(d,_):
            rdma(b.at[t-1,y,zc],b.at[t-1,y,zc],szt.at[t-1,half],rzt.at[t-1,half],z=lax.rem(zc+d,8)).start()
            return 0
        lax.fori_loop(1,8,go,0)
    up=lax.rem(y+1,4); down=lax.rem(y+3,4)
    def slot_a(t,half):
        b=yb[half]
        got(b.at[t-1,0,pl.ds(0,7)],rzt.at[t-1,half])
        for n,d in ((0,up),(1,down)):
            rdma(b.at[t-1,y],b.at[t-1,y],sya.at[t-1,half,n],rya.at[t-1,half,n],y=d).start()
    def slot_b(t,half):
        b=yb[half]
        got(b.at[t-1,0],rya.at[t-1,half,0])
        rdma(b.at[t-1,down,pl.ds(0,4)],b.at[t-1,down,pl.ds(0,4)],syb.at[t-1,half,0],ryb.at[t-1,half,0],y=up).start()
        got(b.at[t-1,0],rya.at[t-1,half,1])
        rdma(b.at[t-1,up,pl.ds(4,4)],b.at[t-1,up,pl.ds(4,4)],syb.at[t-1,half,1],ryb.at[t-1,half,1],y=down).start()
    def slot_done(t):
        for half in range(2):
            b=yb[half]
            got(b.at[t-1,0,pl.ds(0,4)],ryb.at[t-1,half,0])
            got(b.at[t-1,0,pl.ds(0,4)],ryb.at[t-1,half,1])
    def table(t,cap):
        hs=[hat(cap,q) for q in range(16)]
        for h in range(2):
            for c in range(2):
                for v in range(4):
                    acc=None
                    for q in range(16):
                        w=hs[q]*yb[c][t-1,q//4,2*(q%4)+h,:,128*v:128*v+128]
                        acc=w if acc is None else acc+w
                    lk[h*16+c*8:h*16+c*8+8,128*v:128*v+128]=acc

    def sum_a(t,row):
        pay1[t]=row
        in1[t,me_l]=row
        def go(d,_):
            pltpu.make_async_remote_copy(src_ref=pay1.at[t],dst_ref=in1.at[t,me_l],send_sem=s1.at[t],recv_sem=r1.at[t],device_id=line(d),device_id_type=MESH).start()
            return 0
        lax.fori_loop(1,16,go,0)
    def total(buf,t):
        rows=[buf[t,n] for n in range(16)]
        while len(rows)>1:
            rows=[rows[2*n]+rows[2*n+1] for n in range(len(rows)//2)]
        return rows[0]
    def sum_b(t):
        got(in1.at[t,pl.ds(0,15)],r1.at[t])
        row=total(in1,t)
        pay2[t]=row
        in2[t,me_p]=row
        def go(d,_):
            pltpu.make_async_remote_copy(src_ref=pay2.at[t],dst_ref=in2.at[t,me_p],send_sem=s2.at[t],recv_sem=r2.at[t],device_id=plane(d),device_id_type=MESH).start()
            return 0
        lax.fori_loop(1,16,go,0)
    def sum_c(t):
        got(in2.at[t,pl.ds(0,15)],r2.at[t])
        return total(in2,t)
    def mean_of(t,row):
        cap=jnp.sum(row)/1048576.0
        cap_ref[t]=cap
        return cap

    def index(n,_):
        cols=pl.ds(pl.multiple_of(n*1024,1024),1024)
        b=brack_ref[:,cols]; e=shock_ref[:,cols]
        edge=jnp.logical_and(b==511,g==1)
        mine=(b//512)==g
        r=((b//128)%4)*32+e
        ri[:,cols]=jnp.where(mine,r,jnp.where(edge,96+e,-1))
        li[:,cols]=jnp.where(edge,127,b%128)
        own[:,cols]=jnp.where(edge,0.0,1.0)
        fa=b.astype(f32)/1023.0; fb=(b+1).astype(f32)/1023.0
        lo=40.0*fa*fa; hi=40.0*fb*fb
        pbk[:,cols]=lo
        inv[:,cols]=1.0/(hi-lo)
        return 0
    lane=lax.broadcasted_iota(i32,(32,128),1)
    iota=lax.broadcasted_iota(i32,(128,128),0)
    def hot(t):
        def go(n,_):
            for q in range(8):
                cols=pl.ds(pl.multiple_of(n*1024+q*128,128),128)
                o=jnp.where(jnp.broadcast_to(ri[t:t+1,cols],(128,128))==iota,1.0,0.0).astype(jnp.bfloat16)
                oh[t,0:128,cols]=o
                oh[t,128:256,cols]=o
            return 0
        lax.fori_loop(0,8,go,0)
    def shares(t):
        for n in range(8):
            r8=slice(n*8,n*8+8)
            h=hold_ref[r8,:] if t==0 else hp[t-1,r8,:]+hr[t-1,r8,:]
            for q in range(8):
                cols=slice((n*8+q)*128,(n*8+q)*128+128)
                fr_s[t:t+1,cols]=jnp.clip((h[q:q+1,:]-pbk[t:t+1,cols])*inv[t:t+1,cols],0.0,1.0)
    def evolve(t):
        ls=[lk[:,128*v:128*v+128] for v in range(4)]
        ro=[pltpu.roll(q,127,1) for q in ls]
        ds=[jnp.where(lane==127,ro[v+1],ro[v])-ls[v] for v in range(3)]
        last=jnp.where(g==1,ro[0],-ls[3])
        first=jnp.broadcast_to(ls[0][:,0:1],(32,128))
        last=jnp.where(g==1,first,-ls[3])
        ds.append(jnp.where(lane==127,last,ro[3]-ls[3]))
        for o,q in ((0,ls),(128,ds)):
            m=jnp.concatenate(q,axis=0).T
            hi=m.astype(jnp.bfloat16)
            tt[o:o+128,0:128]=hi
            tt[o:o+128,128:256]=(m-hi.astype(f32)).astype(jnp.bfloat16)
        acc=None
        table_now=tt[...]
        for n in range(8):
            rb=res[n%2]
            rb[...]=jnp.dot(table_now,oh[t,:,n*1024:n*1024+1024],preferred_element_type=f32)
            rows=[]
            for q in range(8):
                cols=slice(n*1024+q*128,n*1024+q*128+128)
                m=jnp.broadcast_to(li[t:t+1,cols],(128,128))==iota
                sl=jnp.sum(jnp.where(m,rb[0:128,q*128:q*128+128],0.0),axis=0,keepdims=True)
                sd=jnp.sum(jnp.where(m,rb[128:256,q*128:q*128+128],0.0),axis=0,keepdims=True)
                rows.append(own[t:t+1,cols]*sl+fr_s[t:t+1,cols]*sd)
            hn=jnp.concatenate(rows,axis=0)
            hp[t,n*8:n*8+8,:]=hn
            acc=hn if acc is None else acc+hn
        rdma(hp.at[t],hr.at[t],sh.at[t],rh.at[t],g=1-g).start()
        return jnp.sum(acc,axis=0,keepdims=True)
    def counts(t):
        acc=None
        for n in range(8):
            for q in range(8):
                cols=slice(n*1024+q*128,n*1024+q*128+128)
                m=jnp.broadcast_to(li[t:t+1,cols],(128,128))==iota
                wt[0:128,q*128:q*128+128]=jnp.where(m,jnp.broadcast_to(own[t:t+1,cols],(128,128)),0.0).astype(jnp.bfloat16)
            d=lax.dot_general(oh[t,0:128,n*1024:n*1024+1024],wt[0:128,:],(((1,),(1,)),((),())),preferred_element_type=f32)
            acc=d if acc is None else acc+d
        cl[...]=acc
    def weights(t):
        acc=None
        for n in range(8):
            for q in range(8):
                cols=slice(n*1024+q*128,n*1024+q*128+128)
                m=jnp.broadcast_to(li[t:t+1,cols],(128,128))==iota
                f=jnp.broadcast_to(fr_s[t:t+1,cols],(128,128))
                hi=f.astype(jnp.bfloat16).astype(f32)
                wt[0:128,q*128:q*128+128]=jnp.where(m,hi,0.0).astype(jnp.bfloat16)
                wt[128:256,q*128:q*128+128]=jnp.where(m,f-hi,0.0).astype(jnp.bfloat16)
            d=lax.dot_general(oh[t,0:128,n*1024:n*1024+1024],wt[...],(((1,),(1,)),((),())),preferred_element_type=f32)
            acc=d if acc is None else acc+d
        cd=acc[:,0:128]+acc[:,128:256]
        cs=[cd[32*v:32*v+32,:] for v in range(4)]
        ro=[pltpu.roll(q,1,1) for q in cs]
        for v in range(4):
            if v==3:
                inner=jnp.where(lane==127,0.0,cs[3])
                ctot_v=cl[96:128,:]-inner
                ctot_v=ctot_v-jnp.where(jnp.logical_and(lane==127,g==0),cs[3],0.0)
            else:
                ctot_v=cl[32*v:32*v+32,:]-cs[v]
            prev=ro[v-1] if v else jnp.where(g==1,ro[3],jnp.zeros_like(ro[3]))
            ctot[:,128*v:128*v+128]=ctot_v+jnp.where(lane==0,prev,ro[v])
    lane1=lax.broadcasted_iota(i32,(1,128),1)
    def moments(t,row):
        out=jnp.where(lane1==16,jnp.sum(row,axis=1,keepdims=True),0.0)
        for q in range(16):
            acc=None
            for h in range(2):
                for c in range(2):
                    for v in range(4):
                        w=ctot[h*16+c*8:h*16+c*8+8,128*v:128*v+128]*yb[c][t-1,q//4,2*(q%4)+h,:,128*v:128*v+128]
                        acc=w if acc is None else acc+w
            m=jnp.sum(jnp.sum(acc,axis=0,keepdims=True),axis=1,keepdims=True)
            out=jnp.where(lane1==q,m,out)
        return out

    lax.fori_loop(0,16,pts,0)
    expect()
    for c in inputs[2:]:
        c.wait()
    lax.fori_loop(0,8,index,0)
    h0=jnp.zeros((8,128),f32)
    for n in range(4):
        h0=h0+hold_ref[pl.ds(pl.multiple_of(g*32+n*8,8),8),:]
    pl.semaphore_wait(bar,30)
    expect_a()
    sum_a(0,jnp.sum(h0,axis=0,keepdims=True))
    shares(0)
    hot(0)
    expect_b()
    sum_b(0)
    hot(1)
    hot(2)
    counts(2)
    expect_c()
    bell(0,6)
    row=sum_c(0)
    cap=mean_of(0,row)
    kf=k.astype(f32)
    w0=jnp.maximum(0.0,1.0-jnp.abs(cap-40.0*kf/15)/SP)
    bell(6,8)
    finish(0)
    send_x(0)
    bell(8,10)
    send_y0(0,w0)
    send_slot(1,0)
    bell(10,12)
    finish(1)
    send_x(1)
    send_z0(0)
    send_slot(2,0)
    bell(12,14)
    send_y0(1,w0)
    slot_a(1,0)
    bell(14,16)
    finish(2)
    send_x(2)
    send_z0(1)
    slot_b(1,0)
    send_y0(2,w0)
    send_z0(2)
    send_slot(1,1)
    send_slot(2,1)
    send_slot(3,0)
    send_slot(3,1)
    slot_a(2,0)
    table0(0)
    table0(1)
    table0(2)
    row=evolve(0)
    sum_a(1,row)
    slot_a(1,1)
    slot_b(2,0)
    sum_b(1)
    slot_b(1,1)
    slot_a(2,1)
    slot_a(3,0)
    got(hr.at[0],rh.at[0])
    shares(1)
    hot(3)
    cap=mean_of(1,sum_c(1))
    slot_done(1)
    table(1,cap)
    row=evolve(1)
    slot_b(2,1)
    slot_b(3,0)
    slot_a(3,1)
    got(hr.at[1],rh.at[1])
    shares(2)
    weights(2)
    slot_done(2)
    sum_a(2,moments(2,row))
    sum_b(2)
    slot_b(3,1)
    row=sum_c(2)
    cap=jnp.sum(jnp.where(lane1==16,row,0.0))/1048576.0
    cap_ref[2]=cap
    table(2,cap)
    qs=lane1.astype(f32)*40.0/15
    cap3=jnp.sum(jnp.where(lane1<16,jnp.maximum(0.0,1.0-jnp.abs(cap-qs)/SP)*row,0.0))/1048576.0
    cap_ref[3]=cap3
    evolve(2)
    slot_done(3)
    table(3,cap3)
    got(hr.at[2],rh.at[2])
    shares(3)
    evolve(3)
    got(hr.at[3],rh.at[3])
    h_ref[...]=hp[3]+hr[3]
    got(mid.at[pl.ds(0,7)],sa1)
    got(recv.at[pl.ds(0,15)],sa2)
    for c in range(3):
        got(px[c].at[pl.ds(0,3)],sx.at[c])
        got(y0[c].at[pl.ds(0,3)],sy0.at[c])
        got(z0[c].at[pl.ds(0,7)],sz0.at[c])
    for t in range(3):
        for half in range(2):
            b=yb[half]
            got(b.at[t,0,pl.ds(0,7)],szt.at[t,half])
            for n in range(2):
                got(b.at[t,0],sya.at[t,half,n])
                got(b.at[t,0,pl.ds(0,4)],syb.at[t,half,n])
    for t in range(4):
        got(hp.at[t],sh.at[t])
    for t in range(3):
        got(in1.at[t,pl.ds(0,15)],s1.at[t])
        got(in2.at[t,pl.ds(0,15)],s2.at[t])

def life_call(vt,tw,hold,shock,brack,coef,const,interest,wage,eff,agg):
    vm=pl.BlockSpec(memory_space=pltpu.VMEM); sm=pl.BlockSpec(memory_space=pltpu.SMEM); hb=pl.BlockSpec(memory_space=pl.ANY)
    V=lambda *s: pltpu.VMEM(s,f32)
    B=lambda *s: pltpu.VMEM(s,jnp.bfloat16)
    I=lambda *s: pltpu.VMEM(s,i32)
    S=lambda *s: pltpu.SemaphoreType.DMA(s)
    one=pltpu.SemaphoreType.DMA
    return pl.pallas_call(life,
        out_shape=[jax.ShapeDtypeStruct((16,512),f32),jax.ShapeDtypeStruct((16,512),f32),jax.ShapeDtypeStruct((64,128),f32),jax.ShapeDtypeStruct((4,),f32)],
        in_specs=[hb]*5+[sm]*6,out_specs=[vm,vm,vm,sm],
        scratch_shapes=[V(8,2048),V(128,128),V(64,128),I(4,8192),I(4,8192),V(8,16,1,128),V(8,16,1,128),V(16,8,1,128),
            V(1024,128),V(1024,128),V(1024,512),V(128,128),V(16,8,512),V(16,8,512),
            V(4,8,512),V(4,4,512),V(4,4,512),V(4,8,512),V(4,4,512),V(4,4,512),V(8,8,512),V(8,4,512),V(8,4,512),
            V(3,4,8,8,512),V(3,4,8,8,512),V(32,512),B(256,256),B(4,256,8192),V(256,1024),V(256,1024),
            I(4,8192),I(4,8192),V(4,8192),V(4,8192),V(4,8192),V(4,8192),V(4,64,128),V(4,64,128),V(3,1,128),V(3,16,1,128),V(3,1,128),V(3,16,1,128),
            B(256,1024),V(128,128),V(32,512),
            S(5),one,one,one,one,S(3),S(3),S(3),S(3),S(3),S(3),S(3,2),S(3,2),S(3,2,2),S(3,2,2),S(3,2,2),S(3,2,2),S(4),S(4),S(3),S(3),S(3),S(3)],
        compiler_params=pltpu.CompilerParams(collective_id=1,has_side_effects=True,vmem_limit_bytes=56*1024*1024),name="life")(vt,tw,hold,shock,brack,coef,const,interest,wage,eff,agg)

def put_out(v,p,h,c,vo,po,ho,co,sem):
    copies=[pltpu.make_async_copy(a,b,sem.at[n]) for n,(a,b) in enumerate(((v,vo),(p,po),(h,ho)))]
    for q in copies:
        q.start()
    for n in range(4):
        co[n]=c[n]
    for q in copies:
        q.wait()

def put_out_call(v,p,h,c):
    vm=pl.BlockSpec(memory_space=pltpu.VMEM); sm=pl.BlockSpec(memory_space=pltpu.SMEM); hb=pl.BlockSpec(memory_space=pl.ANY)
    return pl.pallas_call(put_out,out_shape=[jax.ShapeDtypeStruct(a.shape,f32) for a in (v,p,h,c)],in_specs=[vm,vm,vm,sm],out_specs=[hb,hb,hb,sm],
        scratch_shapes=[pltpu.SemaphoreType.DMA((3,))],name="put_out")(v,p,h,c)


def on_device(value_prior,trans_weight,coefficient,constant,interest,wage_level,efficiency,holdings,shocks,brackets,aggregate):
    values_now,policy,final,capital=life_call(value_prior.T,trans_weight,holdings.reshape(64,128),shocks,brackets,coefficient,constant,interest,wage_level,efficiency,aggregate)
    values_now,policy,final,capital=put_out_call(values_now,policy,final,capital)
    return values_now,policy,final.reshape(8192),capital


def solution(mesh):
    finer=Mesh(mesh.devices.reshape(4,4,8,mesh.shape["grid"]),(X,Y,ZC,G))
    in_specs=(P(None,AGENT),P(),P(),P(),P(),P(),P(),P(AGENT),P(None,AGENT),P(None,AGENT),P())
    out_specs=(P(AGENT,G),P(AGENT,G),P(AGENT),P())
    return jax.shard_map(on_device,mesh=finer,in_specs=in_specs,out_specs=out_specs,check_vma=False)
```

time: 123 us -> 98.2 us (0.80)
  Pallas kernels: 118 us -> 97.2 us
  local copies, waits for them, and re-layouts: 4.12 us -> 0 us
    pallas_call x1, Pallas kernels: 22.6 us -> 1.98 us  [put_out_call(): pl.pallas_call(put_out, out_shape=[jax.ShapeDtypeStruct(a.shape, f32) for...]
    unnamed x20 -> x0, local copies, waits for them, and re-layouts: 4.12 us -> none
where the time goes in v2:
time: 98.2 us; the launch traced here: 98 us
  Pallas kernels  97.2 us (99%)
    pallas_call x1, Pallas kernels, life_call(): pl.pallas_call(life, out_shape=[jax.ShapeDtypeStruct((16, 512), f32), jax...  95.2 us
    pallas_call x1, Pallas kernels, put_out_call(): pl.pallas_call(put_out, out_shape=[jax.ShapeDtypeStruct(a.shape, f32) for...  1.98 us

profile of v2, /device:TPU:1, one launch (start us, length us, event | category | flops | bytes accessed | tf_op | source)
XLA Modules:
  0.0 98.0 jit_solution(8741996148771336869)
XLA Ops:
  0.6 95.2 %life.1 = (f32[16,512]{1,0:T(8,128)}, f32[16,512]{1,0:T(8,128)}, f32[64,128]{1,0:T(8,128)}, f32[4]{0:T(128)}) custom-call(f32[8,2048]{1,0:T(8,128)} %bitcast.3, f32[128,128]{1,0:T(8,128)} %tw_hbm.1, f32[64,128]{1,0:T(8,128)} %bitcast.4, s32[4,8192]{1,0:T(4,128)} %shock_hbm.1, s32[4,8192]{1,0:T(4,128)} %brack_hbm.1, f32[4]{0:T(128)} %coef_ref.1, f32[4]{0:T(128)} %const_ref.1, ...), custom_call_target="tpu_custom_call" | custom-call | tf_op jit(solution)/shard_map/life/pallas_call | solution.py:499
  95.8 2.0 %put_out.1 = (f32[16,512]{1,0:T(8,128)}, f32[16,512]{1,0:T(8,128)}, f32[64,128]{1,0:T(8,128)}, f32[4]{0:T(128)}) custom-call(f32[16,512]{1,0:T(8,128)} %get-tuple-element.12.v, f32[16,512]{1,0:T(8,128)} %get-tuple-element.13.p, f32[64,128]{1,0:T(8,128)} %get-tuple-element.14.h, f32[4]{0:T(128)} %get-tuple-element.15.c), custom_call_target="tpu_custom_call" | custom-call | tf_op jit(solution)/shard_map/put_out/pallas_call | solution.py:522

commit v3 on v2

--- a/solution.py
+++ b/solution.py
@@ -13,7 +13,7 @@
 LOG2E=1.4426950408889634
 KT=500.0*LOG2E
 SP=40.0/15
-UN=32
+UN=128
 
 def hat(x,k):
     return jnp.maximum(0.0,1.0-jnp.abs(x-40.0*k/15)/SP)
@@ -26,15 +26,15 @@
     pltpu.make_async_copy(ref,ref,sem).wait()
 
 
-CH=((0,8),(8,4),(12,4))
+CH=((0,8),(8,6),(14,2))
 
 def life(vt_hbm, tw_hbm, hold_hbm, shock_hbm, brack_hbm, coef_ref, const_ref, int_ref, wage_ref, eff_ref, agg_ref,
          v_ref, p_ref, h_ref, cap_ref,
          vt_ref,tw_ref,hold_ref,shock_ref,brack_ref,send,mid,recv,
          pt,kpt,sc,rs,vb,pb,
-         pxa,pxb,pxc,y0a,y0b,y0c,z0a,z0b,z0c,yba,ybb,lk,tt,oh,resa,resb,ri,li,own,pbk,inv,fr_s,hp,hr,pay1,in1,pay2,in2,wt,cl,ctot,
-         sin,sa1,ra1,sa2,ra2,sx,rx,sy0,ry0,sz0,rz0,szt,rzt,sya,rya,syb,ryb,sh,rh,s1,r1,s2,r2):
-    px=(pxa,pxb,pxc); y0=(y0a,y0b,y0c); z0=(z0a,z0b,z0c); yb=(yba,ybb); res=(resa,resb)
+         pxa,pxb,pxc,y0a,y0b,y0c,z0a,z0b,z0c,yba,ybb,ybc,lk,tt,oh,resa,resb,ri,li,own,pbk,inv,fr_s,hp,hr,pay1,in1,pay2,in2,wt,sl,sd,cl,ctot,cp,c1,c2,c3,
+         sin,sa1,ra1,sa2,ra2,sx,rx,sy0,ry0,sz0,rz0,szt,rzt,sya,rya,syb,ryb,sh,rh,s1,r1,s2,r2,sc1,rc1,sc2,rc2,sc3,rc3):
+    px=(pxa,pxb,pxc); y0=(y0a,y0b,y0c); z0=(z0a,z0b,z0c); yb=(yba,ybb,ybc); res=(resa,resb)
     x=lax.axis_index(X); y=lax.axis_index(Y); zc=lax.axis_index(ZC); g=lax.axis_index(G)
     inputs=[pltpu.make_async_copy(a,b,sin.at[n]) for n,(a,b) in enumerate(((vt_hbm,vt_ref),(tw_hbm,tw_ref),(hold_hbm,hold_ref),(shock_hbm,shock_ref),(brack_hbm,brack_ref)))]
     for c in inputs:
@@ -201,11 +201,7 @@
             lk[h*16+a:h*16+a+n,:]=(b[h]+b[2+h])+(b[4+h]+b[6+h])
     def send_slot(t,half):
         b=yb[half]
-        if half==0:
-            b[t-1,y,zc]=px[0][agg_ref[t]]
-        else:
-            b[t-1,y,zc,0:4]=px[1][agg_ref[t]]
-            b[t-1,y,zc,4:8]=px[2][agg_ref[t]]
+        b[t-1,y,zc]=px[half][agg_ref[t]]
         def go(d,_):
             rdma(b.at[t-1,y,zc],b.at[t-1,y,zc],szt.at[t-1,half],rzt.at[t-1,half],z=lax.rem(zc+d,8)).start()
             return 0
@@ -223,20 +219,20 @@
         got(b.at[t-1,0],rya.at[t-1,half,1])
         rdma(b.at[t-1,up,pl.ds(4,4)],b.at[t-1,up,pl.ds(4,4)],syb.at[t-1,half,1],ryb.at[t-1,half,1],y=down).start()
     def slot_done(t):
-        for half in range(2):
+        for half in range(3):
             b=yb[half]
             got(b.at[t-1,0,pl.ds(0,4)],ryb.at[t-1,half,0])
             got(b.at[t-1,0,pl.ds(0,4)],ryb.at[t-1,half,1])
     def table(t,cap):
         hs=[hat(cap,q) for q in range(16)]
         for h in range(2):
-            for c in range(2):
+            for c,(o,n) in enumerate(CH):
                 for v in range(4):
                     acc=None
                     for q in range(16):
                         w=hs[q]*yb[c][t-1,q//4,2*(q%4)+h,:,128*v:128*v+128]
                         acc=w if acc is None else acc+w
-                    lk[h*16+c*8:h*16+c*8+8,128*v:128*v+128]=acc
+                    lk[h*16+o:h*16+o+n,128*v:128*v+128]=acc
 
     def sum_a(t,row):
         pay1[t]=row
@@ -299,11 +295,10 @@
             for q in range(8):
                 cols=slice((n*8+q)*128,(n*8+q)*128+128)
                 fr_s[t:t+1,cols]=jnp.clip((h[q:q+1,:]-pbk[t:t+1,cols])*inv[t:t+1,cols],0.0,1.0)
-    def evolve(t):
+    def gather(t,between=None):
         ls=[lk[:,128*v:128*v+128] for v in range(4)]
         ro=[pltpu.roll(q,127,1) for q in ls]
         ds=[jnp.where(lane==127,ro[v+1],ro[v])-ls[v] for v in range(3)]
-        last=jnp.where(g==1,ro[0],-ls[3])
         first=jnp.broadcast_to(ls[0][:,0:1],(32,128))
         last=jnp.where(g==1,first,-ls[3])
         ds.append(jnp.where(lane==127,last,ro[3]-ls[3]))
@@ -312,18 +307,24 @@
             hi=m.astype(jnp.bfloat16)
             tt[o:o+128,0:128]=hi
             tt[o:o+128,128:256]=(m-hi.astype(f32)).astype(jnp.bfloat16)
-        acc=None
         table_now=tt[...]
         for n in range(8):
+            if n==2 and between is not None:
+                between()
             rb=res[n%2]
             rb[...]=jnp.dot(table_now,oh[t,:,n*1024:n*1024+1024],preferred_element_type=f32)
+            for q in range(8):
+                cols=slice(n*1024+q*128,n*1024+q*128+128)
+                m=jnp.broadcast_to(li[t:t+1,cols],(128,128))==iota
+                sl[:,cols]=own[t:t+1,cols]*jnp.sum(jnp.where(m,rb[0:128,q*128:q*128+128],0.0),axis=0,keepdims=True)
+                sd[:,cols]=jnp.sum(jnp.where(m,rb[128:256,q*128:q*128+128],0.0),axis=0,keepdims=True)
+    def combine(t):
+        acc=None
+        for n in range(8):
             rows=[]
             for q in range(8):
                 cols=slice(n*1024+q*128,n*1024+q*128+128)
-                m=jnp.broadcast_to(li[t:t+1,cols],(128,128))==iota
-                sl=jnp.sum(jnp.where(m,rb[0:128,q*128:q*128+128],0.0),axis=0,keepdims=True)
-                sd=jnp.sum(jnp.where(m,rb[128:256,q*128:q*128+128],0.0),axis=0,keepdims=True)
-                rows.append(own[t:t+1,cols]*sl+fr_s[t:t+1,cols]*sd)
+                rows.append(sl[:,cols]+fr_s[t:t+1,cols]*sd[:,cols])
             hn=jnp.concatenate(rows,axis=0)
             hp[t,n*8:n*8+8,:]=hn
             acc=hn if acc is None else acc+hn
@@ -339,16 +340,18 @@
             d=lax.dot_general(oh[t,0:128,n*1024:n*1024+1024],wt[0:128,:],(((1,),(1,)),((),())),preferred_element_type=f32)
             acc=d if acc is None else acc+d
         cl[...]=acc
-    def weights(t):
+    def weights(t,between=None):
         acc=None
         for n in range(8):
+            if n==4 and between is not None:
+                between()
             for q in range(8):
                 cols=slice(n*1024+q*128,n*1024+q*128+128)
                 m=jnp.broadcast_to(li[t:t+1,cols],(128,128))==iota
-                f=jnp.broadcast_to(fr_s[t:t+1,cols],(128,128))
+                f=fr_s[t:t+1,cols]
                 hi=f.astype(jnp.bfloat16).astype(f32)
-                wt[0:128,q*128:q*128+128]=jnp.where(m,hi,0.0).astype(jnp.bfloat16)
-                wt[128:256,q*128:q*128+128]=jnp.where(m,f-hi,0.0).astype(jnp.bfloat16)
+                wt[0:128,q*128:q*128+128]=jnp.where(m,jnp.broadcast_to(hi,(128,128)),0.0).astype(jnp.bfloat16)
+                wt[128:256,q*128:q*128+128]=jnp.where(m,jnp.broadcast_to(f-hi,(128,128)),0.0).astype(jnp.bfloat16)
             d=lax.dot_general(oh[t,0:128,n*1024:n*1024+1024],wt[...],(((1,),(1,)),((),())),preferred_element_type=f32)
             acc=d if acc is None else acc+d
         cd=acc[:,0:128]+acc[:,128:256]
@@ -367,94 +370,151 @@
     def moments(t,row):
         out=jnp.where(lane1==16,jnp.sum(row,axis=1,keepdims=True),0.0)
         for q in range(16):
-            acc=None
-            for h in range(2):
-                for c in range(2):
+            m=None
+            for c,(o,n) in enumerate(CH):
+                acc=None
+                for h in range(2):
                     for v in range(4):
-                        w=ctot[h*16+c*8:h*16+c*8+8,128*v:128*v+128]*yb[c][t-1,q//4,2*(q%4)+h,:,128*v:128*v+128]
+                        w=ctot[h*16+o:h*16+o+n,128*v:128*v+128]*yb[c][t-1,q//4,2*(q%4)+h,:,128*v:128*v+128]
                         acc=w if acc is None else acc+w
-            m=jnp.sum(jnp.sum(acc,axis=0,keepdims=True),axis=1,keepdims=True)
+                acc=jnp.sum(acc,axis=0,keepdims=True)
+                m=acc if m is None else m+acc
+            m=jnp.sum(m,axis=1,keepdims=True)
             out=jnp.where(lane1==q,m,out)
         return out
 
-    lax.fori_loop(0,16,pts,0)
+    def spread_a():
+        for q in range(8):
+            o=(q%2)*16+(q//2)*4
+            cp[q]=ctot[o:o+4,:]
+        c1[zc]=cp[zc]
+        def go(d,_):
+            o=lax.rem(zc+d,8)
+            rdma(cp.at[o],c1.at[zc],sc1,rc1,z=o).start()
+            return 0
+        lax.fori_loop(1,8,go,0)
+    def added(b,n):
+        rows=[b[q] for q in range(n)]
+        while len(rows)>1:
+            rows=[rows[2*q]+rows[2*q+1] for q in range(len(rows)//2)]
+        return rows[0]
+    def spread_b():
+        got(c1.at[pl.ds(0,7)],rc1)
+        c2[me_p]=added(c1,8)
+        def go(d,_):
+            o=lax.rem(me_p+d,16)
+            rdma(c2.at[me_p],c2.at[me_p],sc2,rc2,x=o//4,y=lax.rem(o,4)).start()
+            return 0
+        lax.fori_loop(1,16,go,0)
+    def spread_c():
+        got(c2.at[pl.ds(0,15)],rc2)
+        c3[zc//2]=added(c2,16)
+        def go(d,_):
+            rdma(c3.at[zc//2],c3.at[zc//2],sc3,rc3,z=lax.rem(zc+2*d,8)).start()
+            return 0
+        lax.fori_loop(1,4,go,0)
+    def first_mean(w):
+        got(c3.at[pl.ds(0,3)],rc3)
+        acc=None
+        for q in range(4):
+            w4=c3[q]*p_ref[q*4:q*4+4,:]
+            acc=w4 if acc is None else acc+w4
+        row=jnp.sum(acc,axis=0,keepdims=True)
+        row=(row[:,0:128]+row[:,128:256])+(row[:,256:384]+row[:,384:512])
+        return row*(w*jnp.where(agg_ref[0]==x,1.0,0.0))
+
     expect()
+    pl.semaphore_wait(bar,30)
+    expect_a()
     for c in inputs[2:]:
         c.wait()
-    lax.fori_loop(0,8,index,0)
     h0=jnp.zeros((8,128),f32)
     for n in range(4):
         h0=h0+hold_ref[pl.ds(pl.multiple_of(g*32+n*8,8),8),:]
-    pl.semaphore_wait(bar,30)
-    expect_a()
     sum_a(0,jnp.sum(h0,axis=0,keepdims=True))
+    lax.fori_loop(0,8,index,0)
     shares(0)
     hot(0)
+    lax.fori_loop(0,16,pts,0)
     expect_b()
+    counts(0)
     sum_b(0)
-    hot(1)
-    hot(2)
-    counts(2)
+    weights(0)
+    spread_a()
     expect_c()
-    bell(0,6)
+    bell(0,4)
     row=sum_c(0)
     cap=mean_of(0,row)
     kf=k.astype(f32)
     w0=jnp.maximum(0.0,1.0-jnp.abs(cap-40.0*kf/15)/SP)
-    bell(6,8)
+    spread_b()
+    bell(4,8)
     finish(0)
     send_x(0)
-    bell(8,10)
+    spread_c()
+    bell(8,11)
     send_y0(0,w0)
     send_slot(1,0)
-    bell(10,12)
+    bell(11,14)
     finish(1)
     send_x(1)
     send_z0(0)
-    send_slot(2,0)
-    bell(12,14)
-    send_y0(1,w0)
-    slot_a(1,0)
     bell(14,16)
     finish(2)
     send_x(2)
+    sum_a(1,first_mean(w0))
+    send_y0(1,w0)
+    send_slot(1,1)
+    hot(1)
+    send_y0(2,w0)
+    send_slot(1,2)
     send_z0(1)
+    slot_a(1,0)
+    send_z0(2)
+    send_slot(2,0)
+    sum_b(1)
+    hot(2)
+    send_slot(2,1)
+    send_slot(2,2)
+    slot_a(1,1)
+    slot_a(1,2)
     slot_b(1,0)
-    send_y0(2,w0)
-    send_z0(2)
-    send_slot(1,1)
-    send_slot(2,1)
-    send_slot(3,0)
-    send_slot(3,1)
-    slot_a(2,0)
     table0(0)
     table0(1)
     table0(2)
-    row=evolve(0)
-    sum_a(1,row)
-    slot_a(1,1)
-    slot_b(2,0)
-    sum_b(1)
-    slot_b(1,1)
+    def later():
+        slot_b(1,1)
+        slot_b(1,2)
+    gather(0,later)
+    combine(0)
+    for n in range(3):
+        send_slot(3,n)
+    cap=mean_of(1,sum_c(1))
+    slot_a(2,0)
+    slot_done(1)
     slot_a(2,1)
-    slot_a(3,0)
+    slot_a(2,2)
+    table(1,cap)
+    gather(1)
     got(hr.at[0],rh.at[0])
     shares(1)
-    hot(3)
-    cap=mean_of(1,sum_c(1))
-    slot_done(1)
-    table(1,cap)
-    row=evolve(1)
-    slot_b(2,1)
-    slot_b(3,0)
-    slot_a(3,1)
+    row=combine(1)
+    counts(2)
+    slot_b(2,0)
     got(hr.at[1],rh.at[1])
     shares(2)
-    weights(2)
+    def later2():
+        slot_b(2,1)
+        slot_b(2,2)
+        for n in range(3):
+            slot_a(3,n)
+    weights(2,later2)
     slot_done(2)
     sum_a(2,moments(2,row))
+    hot(3)
     sum_b(2)
-    slot_b(3,1)
+    for n in range(3):
+        slot_b(3,n)
     row=sum_c(2)
     cap=jnp.sum(jnp.where(lane1==16,row,0.0))/1048576.0
     cap_ref[2]=cap
@@ -462,22 +522,27 @@
     qs=lane1.astype(f32)*40.0/15
     cap3=jnp.sum(jnp.where(lane1<16,jnp.maximum(0.0,1.0-jnp.abs(cap-qs)/SP)*row,0.0))/1048576.0
     cap_ref[3]=cap3
-    evolve(2)
+    gather(2)
+    combine(2)
     slot_done(3)
     table(3,cap3)
+    gather(3)
     got(hr.at[2],rh.at[2])
     shares(3)
-    evolve(3)
+    combine(3)
     got(hr.at[3],rh.at[3])
     h_ref[...]=hp[3]+hr[3]
     got(mid.at[pl.ds(0,7)],sa1)
     got(recv.at[pl.ds(0,15)],sa2)
+    got(c1.at[pl.ds(0,7)],sc1)
+    got(c2.at[pl.ds(0,15)],sc2)
+    got(c3.at[pl.ds(0,3)],sc3)
     for c in range(3):
         got(px[c].at[pl.ds(0,3)],sx.at[c])
         got(y0[c].at[pl.ds(0,3)],sy0.at[c])
         got(z0[c].at[pl.ds(0,7)],sz0.at[c])
     for t in range(3):
-        for half in range(2):
+        for half in range(3):
             b=yb[half]
             got(b.at[t,0,pl.ds(0,7)],szt.at[t,half])
             for n in range(2):
@@ -490,7 +555,7 @@
         got(in2.at[t,pl.ds(0,15)],s2.at[t])
 
 def life_call(vt,tw,hold,shock,brack,coef,const,interest,wage,eff,agg):
-    vm=pl.BlockSpec(memory_space=pltpu.VMEM); sm=pl.BlockSpec(memory_space=pltpu.SMEM); hb=pl.BlockSpec(memory_space=pl.ANY)
+    vm=pl.BlockSpec(memory_space=pltpu.VMEM); sm=pl.BlockSpec(memory_space=pltpu.SMEM); hb=pl.BlockSpec(memory_space=pltpu.HBM)
     V=lambda *s: pltpu.VMEM(s,f32)
     B=lambda *s: pltpu.VMEM(s,jnp.bfloat16)
     I=lambda *s: pltpu.VMEM(s,i32)
@@ -501,12 +566,12 @@
         in_specs=[hb]*5+[sm]*6,out_specs=[vm,vm,vm,sm],
         scratch_shapes=[V(8,2048),V(128,128),V(64,128),I(4,8192),I(4,8192),V(8,16,1,128),V(8,16,1,128),V(16,8,1,128),
             V(1024,128),V(1024,128),V(1024,512),V(128,128),V(16,8,512),V(16,8,512),
-            V(4,8,512),V(4,4,512),V(4,4,512),V(4,8,512),V(4,4,512),V(4,4,512),V(8,8,512),V(8,4,512),V(8,4,512),
-            V(3,4,8,8,512),V(3,4,8,8,512),V(32,512),B(256,256),B(4,256,8192),V(256,1024),V(256,1024),
+            V(4,8,512),V(4,6,512),V(4,2,512),V(4,8,512),V(4,6,512),V(4,2,512),V(8,8,512),V(8,6,512),V(8,2,512),
+            V(3,4,8,8,512),V(3,4,8,6,512),V(3,4,8,2,512),V(32,512),B(256,256),B(4,256,8192),V(256,1024),V(256,1024),
             I(4,8192),I(4,8192),V(4,8192),V(4,8192),V(4,8192),V(4,8192),V(4,64,128),V(4,64,128),V(3,1,128),V(3,16,1,128),V(3,1,128),V(3,16,1,128),
-            B(256,1024),V(128,128),V(32,512),
-            S(5),one,one,one,one,S(3),S(3),S(3),S(3),S(3),S(3),S(3,2),S(3,2),S(3,2,2),S(3,2,2),S(3,2,2),S(3,2,2),S(4),S(4),S(3),S(3),S(3),S(3)],
-        compiler_params=pltpu.CompilerParams(collective_id=1,has_side_effects=True,vmem_limit_bytes=56*1024*1024),name="life")(vt,tw,hold,shock,brack,coef,const,interest,wage,eff,agg)
+            B(256,1024),V(1,8192),V(1,8192),V(128,128),V(32,512),V(8,4,512),V(8,4,512),V(16,4,512),V(4,4,512),
+            S(5),one,one,one,one,S(3),S(3),S(3),S(3),S(3),S(3),S(3,3),S(3,3),S(3,3,2),S(3,3,2),S(3,3,2),S(3,3,2),S(4),S(4),S(3),S(3),S(3),S(3),one,one,one,one,one,one],
+        compiler_params=pltpu.CompilerParams(collective_id=1,has_side_effects=True,vmem_limit_bytes=60*1024*1024),name="life")(vt,tw,hold,shock,brack,coef,const,interest,wage,eff,agg)
 
 def put_out(v,p,h,c,vo,po,ho,co,sem):
     copies=[pltpu.make_async_copy(a,b,sem.at[n]) for n,(a,b) in enumerate(((v,vo),(p,po),(h,ho)))]
@@ -518,8 +583,8 @@
         q.wait()
 
 def put_out_call(v,p,h,c):
-    vm=pl.BlockSpec(memory_space=pltpu.VMEM); sm=pl.BlockSpec(memory_space=pltpu.SMEM); hb=pl.BlockSpec(memory_space=pl.ANY)
-    return pl.pallas_call(put_out,out_shape=[jax.ShapeDtypeStruct(a.shape,f32) for a in (v,p,h,c)],in_specs=[vm,vm,vm,sm],out_specs=[hb,hb,hb,sm],
+    vm=pl.BlockSpec(memory_space=pltpu.VMEM); sm=pl.BlockSpec(memory_space=pltpu.SMEM); hb=pl.BlockSpec(memory_space=pltpu.HBM)
+    return pl.pallas_call(put_out,out_shape=[jax.ShapeDtypeStruct(a.shape,f32) for a in (v,p,h,c)],in_specs=[hb,hb,hb,sm],out_specs=[hb,hb,hb,sm],
         scratch_shapes=[pltpu.SemaphoreType.DMA((3,))],name="put_out")(v,p,h,c)
 
 

time: 98.2 us -> 93.7 us (0.954)
  Pallas kernels: 97.2 us -> 92.7 us
    pallas_call x1, Pallas kernels: 95.2 us -> 87.5 us  [life_call(): pl.pallas_call(life, out_shape=[jax.ShapeDtypeStruct((16, 512), f32), jax...]
    pallas_call x1, Pallas kernels: 1.98 us -> 5.28 us  [put_out_call(): pl.pallas_call(put_out, out_shape=[jax.ShapeDtypeStruct(a.shape, f32) for...]
where the time goes in v3:
time: 93.7 us; the launch traced here: 93.6 us
  Pallas kernels  92.7 us (99%)
    pallas_call x1, Pallas kernels, life_call(): pl.pallas_call(life, out_shape=[jax.ShapeDtypeStruct((16, 512), f32), jax...  87.5 us
    pallas_call x1, Pallas kernels, put_out_call(): pl.pallas_call(put_out, out_shape=[jax.ShapeDtypeStruct(a.shape, f32) for...  5.28 us

profile of v3, /device:TPU:1, one launch (start us, length us, event | category | flops | bytes accessed | tf_op | source)
XLA Modules:
  0.0 93.6 jit_solution(579522587755536936)
XLA Ops:
  0.6 87.5 %life.1 = (f32[16,512]{1,0:T(8,128)}, f32[16,512]{1,0:T(8,128)}, f32[64,128]{1,0:T(8,128)}, f32[4]{0:T(128)}) custom-call(f32[8,2048]{1,0:T(8,128)} %bitcast.3, f32[128,128]{1,0:T(8,128)} %tw_hbm.1, f32[64,128]{1,0:T(8,128)} %bitcast.4, s32[4,8192]{1,0:T(4,128)} %shock_hbm.1, s32[4,8192]{1,0:T(4,128)} %brack_hbm.1, f32[4]{0:T(128)} %coef_ref.1, f32[4]{0:T(128)} %const_ref.1, ...), custom_call_target="tpu_custom_call" | custom-call | tf_op jit(solution)/shard_map/life/pallas_call | solution.py:564
  88.1 5.3 %put_out.1 = (f32[16,512]{1,0:T(8,128)}, f32[16,512]{1,0:T(8,128)}, f32[64,128]{1,0:T(8,128)}, f32[4]{0:T(128)}) custom-call(f32[16,512]{1,0:T(8,128)} %get-tuple-element.12.v, f32[16,512]{1,0:T(8,128)} %get-tuple-element.13.p, f32[64,128]{1,0:T(8,128)} %get-tuple-element.14.h, f32[4]{0:T(128)} %get-tuple-element.15.c), custom_call_target="tpu_custom_call" | custom-call | tf_op jit(solution)/shard_map/put_out/pallas_call | solution.py:587

commit v4 on v3

--- a/solution.py
+++ b/solution.py
@@ -140,7 +140,7 @@
                 D=B-KP
                 for v in range(4):
                     cl=jnp.maximum(W[v]-P,0.1)
-                    S=jnp.log(cl)*(50.0*LOG2E)+jnp.minimum(KW[v]+D,B)
+                    S=lax.log2(cl)*50.0+jnp.minimum(KW[v]+D,B)
                     sc[pl.ds(off,8),128*v:128*v+128]=S
                     M[v]=jnp.maximum(M[v],S)
             return tuple(M)
@@ -309,7 +309,7 @@
             tt[o:o+128,128:256]=(m-hi.astype(f32)).astype(jnp.bfloat16)
         table_now=tt[...]
         for n in range(8):
-            if n==2 and between is not None:
+            if n==3 and between is not None:
                 between()
             rb=res[n%2]
             rb[...]=jnp.dot(table_now,oh[t,:,n*1024:n*1024+1024],preferred_element_type=f32)
@@ -343,7 +343,7 @@
     def weights(t,between=None):
         acc=None
         for n in range(8):
-            if n==4 and between is not None:
+            if n==3 and between is not None:
                 between()
             for q in range(8):
                 cols=slice(n*1024+q*128,n*1024+q*128+128)
@@ -455,6 +455,7 @@
     bell(8,11)
     send_y0(0,w0)
     send_slot(1,0)
+    send_slot(2,0)
     bell(11,14)
     finish(1)
     send_x(1)
@@ -471,41 +472,39 @@
     send_z0(1)
     slot_a(1,0)
     send_z0(2)
-    send_slot(2,0)
     sum_b(1)
-    hot(2)
     send_slot(2,1)
     send_slot(2,2)
+    for n in range(3):
+        send_slot(3,n)
+    slot_a(2,0)
+    hot(2)
     slot_a(1,1)
     slot_a(1,2)
     slot_b(1,0)
     table0(0)
     table0(1)
     table0(2)
-    def later():
-        slot_b(1,1)
-        slot_b(1,2)
-    gather(0,later)
+    gather(0)
     combine(0)
-    for n in range(3):
-        send_slot(3,n)
-    cap=mean_of(1,sum_c(1))
-    slot_a(2,0)
-    slot_done(1)
+    counts(2)
+    slot_b(1,1)
+    slot_b(1,2)
     slot_a(2,1)
     slot_a(2,2)
+    slot_b(2,0)
+    cap=mean_of(1,sum_c(1))
+    slot_done(1)
     table(1,cap)
     gather(1)
     got(hr.at[0],rh.at[0])
     shares(1)
     row=combine(1)
-    counts(2)
-    slot_b(2,0)
     got(hr.at[1],rh.at[1])
     shares(2)
+    slot_b(2,1)
+    slot_b(2,2)
     def later2():
-        slot_b(2,1)
-        slot_b(2,2)
         for n in range(3):
             slot_a(3,n)
     weights(2,later2)
@@ -530,8 +529,6 @@
     got(hr.at[2],rh.at[2])
     shares(3)
     combine(3)
-    got(hr.at[3],rh.at[3])
-    h_ref[...]=hp[3]+hr[3]
     got(mid.at[pl.ds(0,7)],sa1)
     got(recv.at[pl.ds(0,15)],sa2)
     got(c1.at[pl.ds(0,7)],sc1)
@@ -553,6 +550,8 @@
     for t in range(3):
         got(in1.at[t,pl.ds(0,15)],s1.at[t])
         got(in2.at[t,pl.ds(0,15)],s2.at[t])
+    got(hr.at[3],rh.at[3])
+    h_ref[...]=hp[3]+hr[3]
 
 def life_call(vt,tw,hold,shock,brack,coef,const,interest,wage,eff,agg):
     vm=pl.BlockSpec(memory_space=pltpu.VMEM); sm=pl.BlockSpec(memory_space=pltpu.SMEM); hb=pl.BlockSpec(memory_space=pltpu.HBM)
@@ -584,7 +583,7 @@
 
 def put_out_call(v,p,h,c):
     vm=pl.BlockSpec(memory_space=pltpu.VMEM); sm=pl.BlockSpec(memory_space=pltpu.SMEM); hb=pl.BlockSpec(memory_space=pltpu.HBM)
-    return pl.pallas_call(put_out,out_shape=[jax.ShapeDtypeStruct(a.shape,f32) for a in (v,p,h,c)],in_specs=[hb,hb,hb,sm],out_specs=[hb,hb,hb,sm],
+    return pl.pallas_call(put_out,out_shape=[jax.ShapeDtypeStruct(a.shape,f32) for a in (v,p,h,c)],in_specs=[vm,vm,vm,sm],out_specs=[hb,hb,hb,sm],
         scratch_shapes=[pltpu.SemaphoreType.DMA((3,))],name="put_out")(v,p,h,c)
 
 

time: 93.7 us -> 90.1 us (0.962)
  Pallas kernels: 92.7 us -> 89.1 us
    pallas_call x1, Pallas kernels: 5.28 us -> 1.98 us  [put_out_call(): pl.pallas_call(put_out, out_shape=[jax.ShapeDtypeStruct(a.shape, f32) for...]
where the time goes in v4:
time: 90.1 us; the launch traced here: 89.9 us
  Pallas kernels  89.1 us (99%)
    pallas_call x1, Pallas kernels, life_call(): pl.pallas_call(life, out_shape=[jax.ShapeDtypeStruct((16, 512), f32), jax...  87.1 us
    pallas_call x1, Pallas kernels, put_out_call(): pl.pallas_call(put_out, out_shape=[jax.ShapeDtypeStruct(a.shape, f32) for...  1.98 us

profile of v4, /device:TPU:1, one launch (start us, length us, event | category | flops | bytes accessed | tf_op | source)
XLA Modules:
  0.0 89.9 jit_solution(15529179016663355950)
XLA Ops:
  0.6 87.1 %life.1 = (f32[16,512]{1,0:T(8,128)}, f32[16,512]{1,0:T(8,128)}, f32[64,128]{1,0:T(8,128)}, f32[4]{0:T(128)}) custom-call(f32[8,2048]{1,0:T(8,128)} %bitcast.3, f32[128,128]{1,0:T(8,128)} %tw_hbm.1, f32[64,128]{1,0:T(8,128)} %bitcast.4, s32[4,8192]{1,0:T(4,128)} %shock_hbm.1, s32[4,8192]{1,0:T(4,128)} %brack_hbm.1, f32[4]{0:T(128)} %coef_ref.1, f32[4]{0:T(128)} %const_ref.1, ...), custom_call_target="tpu_custom_call" | custom-call | tf_op jit(solution)/shard_map/life/pallas_call | solution.py:563
  87.8 2.0 %put_out.1 = (f32[16,512]{1,0:T(8,128)}, f32[16,512]{1,0:T(8,128)}, f32[64,128]{1,0:T(8,128)}, f32[4]{0:T(128)}) custom-call(f32[16,512]{1,0:T(8,128)} %get-tuple-element.12.v, f32[16,512]{1,0:T(8,128)} %get-tuple-element.13.p, f32[64,128]{1,0:T(8,128)} %get-tuple-element.14.h, f32[4]{0:T(128)} %get-tuple-element.15.c), custom_call_target="tpu_custom_call" | custom-call | tf_op jit(solution)/shard_map/put_out/pallas_call | solution.py:586

commit v5 on v4

--- a/solution.py
+++ b/solution.py
@@ -572,19 +572,16 @@
             S(5),one,one,one,one,S(3),S(3),S(3),S(3),S(3),S(3),S(3,3),S(3,3),S(3,3,2),S(3,3,2),S(3,3,2),S(3,3,2),S(4),S(4),S(3),S(3),S(3),S(3),one,one,one,one,one,one],
         compiler_params=pltpu.CompilerParams(collective_id=1,has_side_effects=True,vmem_limit_bytes=60*1024*1024),name="life")(vt,tw,hold,shock,brack,coef,const,interest,wage,eff,agg)
 
-def put_out(v,p,h,c,vo,po,ho,co,sem):
-    copies=[pltpu.make_async_copy(a,b,sem.at[n]) for n,(a,b) in enumerate(((v,vo),(p,po),(h,ho)))]
-    for q in copies:
-        q.start()
+def put_out(v,p,h,c,vo,po,ho,co):
     for n in range(4):
         co[n]=c[n]
-    for q in copies:
-        q.wait()
+    vo[...]=v[...]
+    po[...]=p[...]
+    ho[...]=h[...]
 
 def put_out_call(v,p,h,c):
-    vm=pl.BlockSpec(memory_space=pltpu.VMEM); sm=pl.BlockSpec(memory_space=pltpu.SMEM); hb=pl.BlockSpec(memory_space=pltpu.HBM)
-    return pl.pallas_call(put_out,out_shape=[jax.ShapeDtypeStruct(a.shape,f32) for a in (v,p,h,c)],in_specs=[vm,vm,vm,sm],out_specs=[hb,hb,hb,sm],
-        scratch_shapes=[pltpu.SemaphoreType.DMA((3,))],name="put_out")(v,p,h,c)
+    vm=pl.BlockSpec(memory_space=pltpu.VMEM); sm=pl.BlockSpec(memory_space=pltpu.SMEM)
+    return pl.pallas_call(put_out,out_shape=[jax.ShapeDtypeStruct(a.shape,f32) for a in (v,p,h,c)],in_specs=[vm,vm,vm,sm],out_specs=[vm,vm,vm,sm],name="put_out")(v,p,h,c)
 
 
 def on_device(value_prior,trans_weight,coefficient,constant,interest,wage_level,efficiency,holdings,shocks,brackets,aggregate):

time: 90.1 us -> 89.6 us (level)
  no operation moved by 1% of the time
where the time goes in v5:
time: 89.6 us; the launch traced here: 89.4 us
  Pallas kernels  88.6 us (99%)
    pallas_call x1, Pallas kernels, life_call(): pl.pallas_call(life, out_shape=[jax.ShapeDtypeStruct((16, 512), f32), jax...  87.1 us

profile of v5, /device:TPU:1, one launch (start us, length us, event | category | flops | bytes accessed | tf_op | source)
XLA Modules:
  0.0 89.4 jit_solution(8298934141224482494)
XLA Ops:
  0.6 87.1 %life.1 = (f32[16,512]{1,0:T(8,128)}, f32[16,512]{1,0:T(8,128)}, f32[64,128]{1,0:T(8,128)}, f32[4]{0:T(128)}) custom-call(f32[8,2048]{1,0:T(8,128)} %bitcast.3, f32[128,128]{1,0:T(8,128)} %tw_hbm.1, f32[64,128]{1,0:T(8,128)} %bitcast.4, s32[4,8192]{1,0:T(4,128)} %shock_hbm.1, s32[4,8192]{1,0:T(4,128)} %brack_hbm.1, f32[4]{0:T(128)} %coef_ref.1, f32[4]{0:T(128)} %const_ref.1, ...), custom_call_target="tpu_custom_call" | custom-call | tf_op jit(solution)/shard_map/life/pallas_call | solution.py:563
  87.8 1.5 %put_out.1 = (f32[16,512]{1,0:T(8,128)}, f32[16,512]{1,0:T(8,128)}, f32[64,128]{1,0:T(8,128)}, f32[4]{0:T(128)}) custom-call(f32[16,512]{1,0:T(8,128)} %get-tuple-element.12.v, f32[16,512]{1,0:T(8,128)} %get-tuple-element.13.p, f32[64,128]{1,0:T(8,128)} %get-tuple-element.14.h, f32[4]{0:T(128)} %get-tuple-element.15.c), custom_call_target="tpu_custom_call" | custom-call | tf_op jit(solution)/shard_map/put_out/pallas_call | solution.py:584
